TPU v7x, 32 devices: a whole 2x2x4 slice. The times are simulated.
32 devices in a mesh: dp: 8 (over z, x), head: 4 (over y, core).
Axes of the slice: x: 2, y: 2, z: 4, core: 2. Of those that a mesh axis runs over, the one named last changes fastest.
Arguments:
- tokens: bfloat16 [11840, 768], P(('dp', 'head')), may hold values from -6 to 6
- caption_len: int32 [64], P('dp'), may hold values from 5 to 40, as said below
- first_gain: bfloat16 [768], P(('dp', 'head')), may hold values from 0.5 to 1.5
- first_shift: bfloat16 [768], P(('dp', 'head')), may hold values from -3 to 3
- qkv_weight: bfloat16 [768, 3, 768], P('dp', None, 'head'), may hold values from -0.21875 to 0.21875
- qkv_bias: bfloat16 [2, 768], P(None, ('head', 'dp')), may hold values from -3 to 3
- out_weight: bfloat16 [768, 768], P(('dp', 'head')), may hold values from -1.25 to 1.25
- out_bias: bfloat16 [768], P(('dp', 'head')), may hold values from -3 to 3
- second_gain: bfloat16 [768], P(('dp', 'head')), may hold values from 0.5 to 1.5
- second_shift: bfloat16 [768], P(('dp', 'head')), may hold values from -3 to 3
- up_weight: bfloat16 [768, 3072], P('dp', 'head'), may hold values from -0.21875 to 0.21875
- up_bias: bfloat16 [3072], P(('head', 'dp')), may hold values from -3 to 3
- down_weight: bfloat16 [3072, 768], P('head', 'dp'), may hold values from -0.109375 to 0.109375
- down_bias: bfloat16 [768], P(('dp', 'head')), may hold values from -3 to 3
- output_grad: bfloat16 [11840, 768], P(('dp', 'head')), may hold values from -6 to 6
Outputs:
- layer_out: bfloat16 [11840, 768], P(('dp', 'head'))
- tokens_grad: bfloat16 [11840, 768], P(('dp', 'head'))
- first_gain_grad: float32 [768], P(('dp', 'head'))
- first_shift_grad: float32 [768], P(('dp', 'head'))
- qkv_weight_grad: float32 [768, 3, 768], P('dp', None, 'head')
- qkv_bias_grad: float32 [2, 768], P(None, ('head', 'dp'))
- out_weight_grad: float32 [768, 768], P(('dp', 'head'))
- out_bias_grad: float32 [768], P(('dp', 'head'))
- second_gain_grad: float32 [768], P(('dp', 'head'))
- second_shift_grad: float32 [768], P(('dp', 'head'))
- up_weight_grad: float32 [768, 3072], P('dp', 'head')
- up_bias_grad: float32 [3072], P(('head', 'dp'))
- down_weight_grad: float32 [3072, 768], P('head', 'dp')
- down_bias_grad: float32 [768], P(('dp', 'head'))
Inputs may be any that keep to these rules, and one draw needn't show every extreme that they name: Each pair's caption fills its first caption_len slots; some pair's caption fills all 40 slots.
All inputs are finite; a program needn't handle non-finite values.
Results may differ from a plain program's by a relative error of at most 0.014.
Values may be sent and summed in bfloat16 or wider, within the bound.
No kernel may reach another device: no remote copies, remote signals or barrier semaphores. Data moves between devices by JAX's collectives and lax.ppermute only.
A program may use at most 128 MiB of HBM per device.

v0:
```python
import functools
import math

import jax
import jax.numpy as jnp
from jax import lax
from jax.experimental.layout import Layout, with_layout_constraint
from jax.experimental import pallas as pl
from jax.experimental.pallas import tpu as pltpu
from jax.sharding import PartitionSpec as P

HEAD_DIM = 64
TEXT = 40
ALL = ("dp", "head")
F32 = jnp.float32
BF16 = jnp.bfloat16


def mm(a, b):
    return jnp.dot(a, b, preferred_element_type=F32)


def mm_t(a, b):
    return lax.dot_general(a, b, (((1,), (1,)), ((), ())), preferred_element_type=F32)


def t_mm(a, b):
    return lax.dot_general(a, b, (((0,), (0,)), ((), ())), preferred_element_type=F32)


def norm_parts(values):
    spread = values - jnp.mean(values, axis=-1, keepdims=True)
    root = lax.rsqrt(jnp.mean(spread * spread, axis=-1, keepdims=True) + 1e-06)
    return spread * root, root


def norm_back(grad, gain, hat, root):
    scaled = grad * gain
    first = jnp.mean(scaled, axis=-1, keepdims=True)
    second = jnp.mean(scaled * hat, axis=-1, keepdims=True)
    return root * (scaled - first - hat * second)


VMEM = pltpu.VMEM


def spec(shape, index):
    return pl.BlockSpec(shape, index, memory_space=VMEM)


def whole(shape):
    return spec(shape, lambda *_: (0,) * len(shape))


def chunk(shape):
    return spec((1,) + shape, lambda j, *_: (j,) + (0,) * len(shape))


def nearer(t, near, far):
    return jnp.where(t < pl.num_programs(0) // 2, near[0], far[0])


def store(t, near, far, value):
    half = pl.num_programs(0) // 2

    @pl.when(t < half)
    def _():
        near[0] = value

    @pl.when(t >= half)
    def _():
        far[0] = value


def column_sum(matrix):
    return jnp.sum(matrix.astype(F32), axis=0, keepdims=True)


def counting(shape, axis):
    return lax.broadcasted_iota(jnp.int32, shape, axis)


def repeats(part, size):
    return (counting((part, size), 1) % part == counting((part, size), 0)).astype(F32)


def owners(devices, part, size):
    return counting((devices, size), 1) // part, counting((devices, size), 0)


def spread_vectors(per, order, smalls, turn, vectors, b_qv, b_up):
    devices, width = smalls.shape[0], turn.shape[0]
    chunks, _, part = b_up.shape
    values = smalls[...].astype(F32)
    plain = vectors.shape[0]
    pattern = repeats(per, width).astype(BF16)
    block, device = owners(devices, per, width)
    rows = []
    for v in range(plain):
        row = mm(values[:, v * per : (v + 1) * per].astype(BF16), pattern)
        rows.append(jnp.sum(jnp.where(block == device, row, 0.0), axis=0, keepdims=True))
    vectors[...] = mm(jnp.concatenate(rows, axis=0).astype(BF16), turn[...])

    def by_chunk(first, size, length, out):
        tall = mm(
            values[:, first : first + size].astype(BF16), repeats(size, length).astype(BF16)
        )
        block, device = owners(devices, size, length)
        for t in range(chunks):
            mine = device == block * chunks + order[t]
            out(t, jnp.sum(jnp.where(mine, tall, 0.0), axis=0, keepdims=True))

    def set_query(t, row):
        b_qv[t, 0:1, :] = row

    def set_value(t, row):
        b_qv[t, 1:2, :] = row

    def set_up(t, row):
        b_up[t] = row

    cols = b_qv.shape[2]
    by_chunk(plain * per, per, cols, set_query)
    by_chunk((plain + 1) * per, per, cols, set_value)
    by_chunk((plain + 2) * per, values.shape[1] - (plain + 2) * per, part, set_up)


def collect_vectors(per, order, sums_one, sums_two, g_b, g_bu, turn, out):
    devices, width = out.shape[0], turn.shape[0]
    chunks, _, part = g_bu.shape

    def exact(a, b):
        high = a.astype(BF16)
        left = a - high.astype(F32)
        mid = left.astype(BF16)
        low = (left - mid.astype(F32)).astype(BF16)
        count = a.shape[0]
        parts = mm_t(jnp.concatenate([part.astype(F32) for part in (high, mid, low)]).astype(BF16), b)
        return parts[:count] + (parts[count : 2 * count] + parts[2 * count :])

    plain = sums_one.shape[0] + sums_two.shape[0]
    rows = jnp.concatenate([sums_one[...], sums_two[...]], axis=0)
    rows = exact(rows, turn[...])
    block, device = owners(devices, per, width)
    tall = [jnp.where(block == device, rows[v : v + 1, :], 0.0) for v in range(plain)]
    tall = exact(jnp.concatenate(tall, axis=0), repeats(per, width).astype(BF16))
    columns = [tall[v * devices : (v + 1) * devices, :] for v in range(plain)]

    def by_chunk(row_of, size, length):
        block, device = owners(devices, size, length)
        tall = jnp.zeros((devices, length), F32)
        for t in range(chunks):
            tall = jnp.where(device == block * chunks + order[t], row_of(t), tall)
        columns.append(exact(tall, repeats(size, length).astype(BF16)))

    cols = g_b.shape[2] // 3
    by_chunk(lambda t: g_b[t][:, :cols], per, cols)
    by_chunk(lambda t: g_b[t][:, 2 * cols :], per, cols)
    by_chunk(lambda t: g_bu[t], out.shape[1] - (plain + 2) * per, part)
    out[...] = jnp.concatenate(columns, axis=1)


def attention_forward(
    items,
    seq,
    lengths,
    order,
    x,
    vectors,
    qk_near,
    qk_far,
    vo_near,
    vo_far,
    b_qv,
    out_q,
    out_k,
    out_v,
    out_p,
    out_c,
    normed,
):
    t = pl.program_id(0)
    rows = x.shape[0] // items
    cols = out_q.shape[2]
    scale = HEAD_DIM**-0.5

    @pl.when(t == 0)
    def _():
        def some(span, nothing):
            hat, _ = norm_parts(x[span, :].astype(F32))
            normed[span, :] = (hat * vectors[0:1, :] + vectors[1:2, :]).astype(BF16)
            return nothing

        by_rows(x.shape[0], 0, some)

    bias = b_qv[t]
    both = mm(normed[...], nearer(t, qk_near, qk_far))
    query = (both[:, :cols] + bias[0:1, :]).astype(BF16)
    key = both[:, cols:].astype(BF16)
    value = (mm(normed[...], nearer(t, vo_near, vo_far)[:, :cols]) + bias[1:2, :]).astype(BF16)
    out_q[0] = query
    out_k[0] = key
    out_v[0] = value
    heads = cols // HEAD_DIM
    at = lax.broadcasted_iota(jnp.int32, (rows, rows), 1)
    jobs = [
        (item, head, slice(item * rows, (item + 1) * rows))
        for item in range(items)
        for head in range(heads)
    ]
    visible = [((at >= TEXT) & (at < seq)) | (at < lengths[item]) for item in range(items)]

    def lanes(head):
        return slice(head * HEAD_DIM, (head + 1) * HEAD_DIM)

    scores = [
        mm_t(query[mine, lanes(head)], key[mine, lanes(head)]) * scale for _, head, mine in jobs
    ]
    parts = []
    for (item, head, _), score in zip(jobs, scores):
        score = jnp.where(visible[item], score, -1000000000.0)
        raised = jnp.exp(score - jnp.max(score, axis=-1, keepdims=True))
        probs = raised / jnp.sum(raised, axis=-1, keepdims=True)
        out_p[0, item * heads + head] = probs
        parts.append(probs.astype(BF16))
    parts = [mm(low, value[mine, lanes(head)]) for (_, head, mine), low in zip(jobs, parts)]
    for item in range(items):
        mine = slice(item * rows, (item + 1) * rows)
        whole_item = jnp.concatenate(parts[item * heads : (item + 1) * heads], axis=1)
        out_c[0, mine, :] = whole_item.astype(BF16)


def by_rows(count, carry, body):
    part = math.gcd(count, 128)

    def one(i, carry):
        return body(pl.ds(pl.multiple_of(i * part, part), part), carry)

    return lax.fori_loop(0, count // part, one, carry)


def chunk_rows(order, c, cols):
    return pl.ds(pl.multiple_of(order[c] * cols, cols), cols)


def between(order, x, ctx, w_out, vectors, top, middle, hidden, hidden_t, top_t):
    chunks, _, cols = ctx.shape
    total = x[...].astype(F32) + vectors[2:3, :]
    for c in range(chunks):
        total += mm(ctx[c], w_out[chunk_rows(order, c, cols), :])
    middle[...] = total

    def some(span, nothing):
        hat, _ = norm_parts(middle[span, :])
        low = hat * vectors[3:4, :] + vectors[4:5, :]
        hidden[span, :] = low.astype(BF16)
        hidden_t[:, span] = low.T.astype(BF16)
        top_t[:, span] = top[span, :].astype(F32).T.astype(BF16)
        return nothing

    by_rows(x.shape[0], 0, some)


def feed_forward(last, hidden, hidden_t, top, top_t, *rest):
    ups, downs, b_up, rest = rest[:4], rest[4:8], rest[8], rest[9:]
    late = []
    if last:
        order, vectors, *late = rest[:6]
        rest = rest[6:]
    grads_out, out_bu, rest = rest[:4], rest[4], rest[5:]
    if last:
        out_y, out_gm, out_ga, out_gc, out_sums, *rest = rest
    sum_y, sum_h, weights, grads, in_sems, out_sems, *late_here = rest
    half = weights.shape[2] // 2

    loads = []
    for i, piece in enumerate(ups + downs):
        here = weights.at[i // 2 % 2, i // 4, pl.ds(i % 2 * half, half)]
        loads.append(pltpu.make_async_copy(piece, here, in_sems.at[i]))
    for i, (piece, here) in enumerate(zip(late, late_here)):
        loads.append(pltpu.make_async_copy(piece, here, in_sems.at[8 + i]))
    near_loads = loads[:2] + loads[4:6]
    far_loads = loads[2:4] + loads[6:]
    for load in near_loads + far_loads:
        load.start()
    sends = [
        pltpu.make_async_copy(grads.at[i % 2, i // 2], grads_out[i], out_sems.at[i])
        for i in range(4)
    ]
    sum_y[...] = jnp.zeros_like(sum_y)
    sum_h[...] = jnp.zeros_like(sum_h)

    def work(which, nothing):
        @pl.when(which == 0)
        def _():
            for load in near_loads:
                load.wait()

        @pl.when(which == 1)
        def _():
            for load in far_loads:
                load.wait()

        w_up, w_down_t = weights[which, 0], weights[which, 1]
        up = mm(hidden[...], w_up) + b_up[which]
        phi = 0.5 * (1.0 + lax.erf(up * (0.5**0.5)))
        active = (up * phi).astype(BF16)
        slope = phi + up * jnp.exp(-0.5 * up * up) * ((2.0 * jnp.pi) ** -0.5)
        grad_up = (mm(top[...], w_down_t) * slope).astype(BF16)
        grads[which, 1] = mm(top_t[...], active).astype(BF16)
        grads[which, 0] = mm(hidden_t[...], grad_up).astype(BF16)

        @pl.when(which == 0)
        def _():
            sends[0].start()
            sends[2].start()

        @pl.when(which == 1)
        def _():
            sends[1].start()
            sends[3].start()

        out_bu[which] = column_sum(grad_up)
        sum_y[...] += mm_t(active, w_down_t)
        sum_h[...] += mm_t(grad_up, w_up)
        return nothing

    lax.fori_loop(0, 2, work, 0)
    if last:
        middle, w_out, in_y, in_h = late_here
        chunks, _, cols = out_gc.shape
        gain = vectors[3:4, :]
        zero = jnp.zeros((1, out_y.shape[1]), F32)

        def some(span, sums):
            hat, root = norm_parts(middle[span, :])
            total_y = in_y[span, :] + sum_y[span, :]
            out_y[span, :] = (middle[span, :] + (total_y + vectors[5:6, :])).astype(BF16)
            grad_hidden = in_h[span, :] + sum_h[span, :]
            grad_top = top[span, :].astype(F32)
            grad_middle = grad_top + norm_back(grad_hidden, gain, hat, root)
            out_gm[span, :] = grad_middle
            grad_attn = grad_middle.astype(BF16)
            out_ga[span, :] = grad_attn
            fresh = grad_attn, grad_hidden * hat, grad_hidden, grad_top
            return tuple(one + column_sum(other) for one, other in zip(sums, fresh))

        sums = by_rows(out_y.shape[0], (zero,) * 4, some)
        out_sums[...] = jnp.concatenate(sums, axis=0)
        grad_attn = out_ga[...]

        def one_chunk(c, nothing):
            out_gc[c] = mm_t(grad_attn, w_out[chunk_rows(order, c, cols), :]).astype(BF16)
            return nothing

        lax.fori_loop(0, chunks, one_chunk, 0)
    for send in sends:
        send.wait()


def out_gradient(order, ctx, grad_attn, turn, out_go):
    chunks, _, cols = ctx.shape

    def one_chunk(c, nothing):
        grad_out = t_mm(ctx[c], grad_attn[...]).astype(BF16)
        out_go[chunk_rows(order, c, cols), :] = mm_t(grad_out, turn[...]).astype(BF16)
        return nothing

    lax.fori_loop(0, chunks, one_chunk, 0)


def attention_backward(
    items,
    x,
    vectors,
    qk_near,
    qk_far,
    vo_near,
    vo_far,
    query,
    key,
    value,
    probs,
    grad_ctx,
    grad_middle,
    out_x,
    gqk_near,
    gqk_far,
    gvo_near,
    gvo_far,
    out_b,
    out_sums,
    hat,
    root,
    normed_t,
    sum_n,
):
    rows = x.shape[0] // items
    cols = query.shape[2]
    heads = cols // HEAD_DIM
    scale = HEAD_DIM**-0.5
    t = pl.program_id(0)
    gain = vectors[0:1, :]

    @pl.when(t == 0)
    def _():
        def some(span, nothing):
            hat_one, root_one = norm_parts(x[span, :].astype(F32))
            hat[span, :] = hat_one
            root[span, :] = root_one
            normed_t[:, span] = (hat_one * gain + vectors[1:2, :]).T.astype(BF16)
            return nothing

        by_rows(x.shape[0], 0, some)
        sum_n[...] = jnp.zeros_like(sum_n)

    jobs = [
        (item, head, slice(item * rows, (item + 1) * rows))
        for item in range(items)
        for head in range(heads)
    ]

    def lanes(head):
        return slice(head * HEAD_DIM, (head + 1) * HEAD_DIM)

    grads_p = [
        mm_t(grad_ctx[0, mine, lanes(head)], value[0, mine, lanes(head)]) for _, head, mine in jobs
    ]
    parts_v = [
        t_mm(probs[0, item * heads + head].astype(BF16), grad_ctx[0, mine, lanes(head)])
        for item, head, mine in jobs
    ]
    grads_s = []
    for (item, head, _), grad_p in zip(jobs, grads_p):
        p = probs[0, item * heads + head]
        row = jnp.sum(p * grad_p, axis=-1, keepdims=True)
        grads_s.append((p * (grad_p - row)).astype(BF16))
    parts_q = [
        mm(grad_s, key[0, mine, lanes(head)]) * scale for (_, head, mine), grad_s in zip(jobs, grads_s)
    ]
    parts_k = [
        t_mm(grad_s, query[0, mine, lanes(head)]) * scale
        for (_, head, mine), grad_s in zip(jobs, grads_s)
    ]

    def gathered(parts):
        items_of = [
            jnp.concatenate(parts[item * heads : (item + 1) * heads], axis=1)
            for item in range(items)
        ]
        return jnp.concatenate(items_of, axis=0).astype(BF16)

    grad_all = jnp.concatenate([gathered(p) for p in (parts_q, parts_k, parts_v)], axis=1)
    out_b[0] = column_sum(grad_all)
    grad_qk, grad_v = grad_all[:, : 2 * cols], grad_all[:, 2 * cols :]
    store(t, gqk_near, gqk_far, mm(normed_t[...], grad_qk).astype(BF16))
    grad_weight = mm(normed_t[...], grad_v).astype(BF16)
    store(t, gvo_near, gvo_far, grad_weight)
    sum_n[...] += mm_t(grad_qk, nearer(t, qk_near, qk_far))
    sum_n[...] += mm_t(grad_v, nearer(t, vo_near, vo_far)[:, :cols])

    @pl.when(t == pl.num_programs(0) - 1)
    def _():
        zero = jnp.zeros((1, x.shape[1]), F32)

        def some(span, sums):
            grad_normed = sum_n[span, :]
            back = norm_back(grad_normed, gain, hat[span, :], root[span, :])
            out_x[span, :] = (grad_middle[span, :] + back).astype(BF16)
            fresh = grad_normed * hat[span, :], grad_normed
            return tuple(one + column_sum(other) for one, other in zip(sums, fresh))

        out_sums[...] = jnp.concatenate(by_rows(x.shape[0], (zero,) * 2, some), axis=0)


def call(body, grid, in_specs, outs, scratch, flops, moved, *args):
    return pl.pallas_call(
        body,
        grid=grid,
        in_specs=in_specs,
        out_specs=[o[1] for o in outs],
        out_shape=[jax.ShapeDtypeStruct(*o[0]) for o in outs],
        scratch_shapes=scratch,
        compiler_params=pltpu.CompilerParams(
            dimension_semantics=("arbitrary",) * len(grid), vmem_limit_bytes=60 * 1024 * 1024
        ),
        cost_estimate=pl.CostEstimate(flops=flops // 8, bytes_accessed=moved // 8, transcendentals=0),
    )(*args)


def local(
    n_dp,
    n_head,
    tokens,
    caption_len,
    first_gain,
    first_shift,
    qkv_weight,
    qkv_bias,
    out_weight,
    out_bias,
    second_gain,
    second_shift,
    up_weight,
    up_bias,
    down_weight,
    down_bias,
    output_grad,
):
    rows, width = tokens.shape
    hidden = up_weight.shape[1] * n_head
    devices = n_dp * n_head
    item_count = caption_len.shape[0] // n_head
    seq = rows // item_count
    dp_bits = [("dp", 1 << i) for i in reversed(range(n_dp.bit_length() - 1))]
    head_bits = [("head", 1 << i) for i in reversed(range(n_head.bit_length() - 1))]
    held = (dp_bits + head_bits)[::-1]
    along_z, along_x, along_y = dp_bits[:-1], dp_bits[-1:], head_bits[:-1]
    core = head_bits[-1]

    def flip(piece, step):
        axis, bit = step
        count = n_dp if axis == "dp" else n_head
        rows_first = Layout(tuple(range(piece.ndim)))
        piece = with_layout_constraint(piece, rows_first)
        piece = lax.ppermute(piece, axis, [(i, i ^ bit) for i in range(count)])
        return with_layout_constraint(piece, rows_first)

    def together(*values):
        return lax.optimization_barrier(values)

    def place_of(step, have):
        return sum(held.index(h) < held.index(step) for h in have)

    def grow(piece, step, have):
        other = flip(piece, step)
        piece = jnp.stack([piece, other], axis=place_of(step, have))
        have.append(step)
        return piece

    def both(step, other):
        return step[0], step[1] | other[1]

    def grow_two(piece, step, other, have):
        pieces = [piece, flip(piece, step), flip(piece, other), flip(piece, both(step, other))]
        have.extend([step, other])
        return jnp.stack(pieces).reshape((2, 2) + piece.shape)

    def side(terms, which, place):
        return [lax.index_in_dim(term, which, place, False) for term in terms]

    def total(terms):
        return sum(term.astype(F32) for term in terms)

    def shrink(terms, step, have):
        place = have.index(step)
        have.remove(step)
        away = total(side(terms, 1, place)).astype(BF16)
        return side(terms, 0, place) + [flip(away, step)]

    def reverse_bits(value, count):
        return sum(
            ((value >> i) & 1) << (count.bit_length() - 2 - i) for i in range(count.bit_length() - 1)
        )

    my_dp, my_head = lax.axis_index("dp"), lax.axis_index("head")
    order_chunks = my_head ^ reverse_bits(jnp.arange(n_head, dtype=jnp.int32), n_head)
    order_blocks = my_dp ^ reverse_bits(jnp.arange(n_dp, dtype=jnp.int32), n_dp)

    def exchange(blocks):
        return lax.all_to_all(blocks, ALL, 0, 0, tiled=True)

    per = first_gain.shape[0]
    smem = pl.BlockSpec(memory_space=pltpu.SMEM)
    pieces = [first_gain, first_shift, out_bias, second_gain, second_shift, down_bias]
    pieces += [qkv_bias[0], qkv_bias[1], up_bias]
    small_size = sum(piece.shape[0] for piece in pieces)
    smalls, start = 0, 0
    for piece in pieces:
        stop = start + piece.shape[0]
        smalls += jnp.pad(piece, (start, small_size - stop))
        start = stop
    part_rows = width // n_dp
    part_cols = width // n_head
    part_hidden = up_weight.shape[1]
    part_hidden = up_weight.shape[1]
    features = jnp.arange(width, dtype=jnp.int32)
    place = jnp.repeat(order_blocks, part_rows) * part_rows + features % part_rows
    turn = (features[:, None] == place[None, :]).astype(BF16)

    def turned(piece):
        return mm(piece, turn).astype(BF16)

    def turned_back(piece):
        return mm_t(piece, turn).astype(BF16)

    ranks = order_blocks[None, :] * n_head + order_chunks[:, None]
    ranks = ranks.reshape(-1)
    chunk_of = reverse_bits(my_head ^ jnp.arange(n_head, dtype=jnp.int32), n_head)
    block_of = reverse_bits(my_dp ^ jnp.arange(n_dp, dtype=jnp.int32), n_dp)
    ranks_back = (chunk_of[None, :] * n_dp + block_of[:, None]).reshape(-1)
    padded = -(-seq // 16) * 16
    total_rows = item_count * padded

    def pad(piece):
        piece = piece.reshape(item_count, seq, width)
        return jnp.pad(piece, ((0, 0), (0, padded - seq), (0, 0))).reshape(total_rows, width)

    def unpad(piece):
        return piece.reshape(item_count, padded, width)[:, :seq].reshape(rows, width)

    def out_pack(piece):
        return piece.reshape(-1, n_head, part_cols).transpose(1, 0, 2).reshape(part_rows, part_cols)

    have, have_rest = [], []
    first = [qkv_weight.reshape(part_rows, 3 * part_cols), out_pack(out_weight)]
    first = jnp.concatenate(first, axis=1)
    rest = jnp.concatenate([up_weight, down_weight.T])
    for step in along_z[:-2]:
        first = grow(first, step, have)
    first = grow_two(first, *along_z[-2:], have)
    x, top = turned(pad(tokens)), turned(pad(output_grad))
    smalls = exchange(jnp.broadcast_to(smalls[None], (devices,) + smalls.shape))
    first, rest, x, top, smalls = together(first, rest, x, top, smalls)

    part_cols = width // n_head
    vectors, b_qv, b_up = call(
        functools.partial(spread_vectors, per),
        (1,),
        [smem, whole(smalls.shape), whole((width, width))],
        [
            (((6, width), F32), whole((6, width))),
            (((n_head, 2, part_cols), F32), whole((n_head, 2, part_cols))),
            (((n_head, 1, hidden // n_head), F32), whole((n_head, 1, hidden // n_head))),
        ],
        [],
        0,
        4 * width * width,
        order_chunks,
        smalls,
        turn,
    )
    w_qk, w_vo = first[..., : 2 * part_cols], first[..., 2 * part_cols :]
    have_qk, have_vo = list(have), list(have)
    w_qk, w_vo = grow(w_qk, along_x[0], have_qk), grow(w_vo, along_y[0], have_vo)
    rest = grow(rest, along_z[0], have_rest)
    w_qk, w_vo, rest, vectors, b_qv, b_up = together(w_qk, w_vo, rest, vectors, b_qv, b_up)
    for step in along_z[1:-1]:
        rest = grow(rest, step, have_rest)
    for step in along_y[:-1]:
        w_qk = grow(w_qk, step, have_qk)
    for step in along_y[1:]:
        w_vo = grow(w_vo, step, have_vo)
    w_qk, w_vo = grow(w_qk, along_y[-1], have_qk), grow(w_vo, along_x[0], have_vo)
    rest = grow(rest, along_z[-1], have_rest)
    w_up, w_down = rest[..., :part_rows, :], rest[..., part_rows:, :]
    pair_shape = (-1, width, 2 * part_cols)
    near_qk, near_vo, w_up, w_down = together(
        w_qk.reshape(pair_shape), w_vo.reshape(pair_shape), w_up, w_down
    )
    far_qk, far_vo = flip(near_qk, core), flip(near_vo, core)
    step_x, step_y = along_x[0], along_y[0]
    up_x, down_x = flip(w_up, step_x), flip(w_down, step_x)
    up_y, down_y = flip(w_up, step_y), flip(w_down, step_y)


    lengths = lax.dynamic_slice_in_dim(caption_len, my_head * item_count, item_count)
    pairs = item_count * (part_cols // HEAD_DIM)

    full = (total_rows, width)
    slab = (total_rows, part_cols)
    slab_out = (((n_head,) + slab, BF16), chunk(slab))
    probs_out = (((n_head, pairs, padded, padded), F32), chunk((pairs, padded, padded)))
    weights = width * width

    half = n_head // 2

    def near(shape):
        return spec((1,) + shape, lambda t: (jnp.minimum(t, half - 1), 0, 0))

    def far(shape):
        return spec((1,) + shape, lambda t: (jnp.maximum(t - half, 0), 0, 0))

    two_cols, one_col = (width, 2 * part_cols), (width, part_cols)
    first_specs = [near(two_cols), far(two_cols)] * 2
    query, key, value, probs, context = call(
        functools.partial(attention_forward, item_count, seq),
        (n_head,),
        [smem, smem, whole(full), whole(vectors.shape)]
        + first_specs
        + [whole(b_qv.shape)],
        [slab_out, slab_out, slab_out, probs_out, slab_out],
        [pltpu.VMEM(full, BF16)],
        8 * total_rows * weights,
        12 * weights,
        lengths,
        order_chunks,
        x,
        vectors,
        near_qk,
        far_qk,
        near_vo,
        far_vo,
        b_qv,
    )

    w_out = jnp.concatenate([near_vo[..., part_cols:], far_vo[..., part_cols:]])
    w_out = w_out.reshape(devices, n_head, -1, part_cols).transpose(0, 2, 1, 3)
    w_out = w_out.reshape(devices, -1, width)
    w_out = turned(w_out[ranks_back].reshape(width, width))
    middle, low, low_t, top_t = call(
        between,
        (1,),
        [smem, whole(full), whole((n_head,) + slab), whole((width, width))]
        + [whole(vectors.shape), whole(full)],
        [
            ((full, F32), whole(full)),
            ((full, BF16), whole(full)),
            ((full[::-1], BF16), whole(full[::-1])),
            ((full[::-1], BF16), whole(full[::-1])),
        ],
        [],
        2 * total_rows * weights,
        8 * weights,
        order_chunks,
        x,
        context,
        w_out,
        vectors,
        top,
    )

    up_x, down_x, up_y, down_y, low = together(up_x, down_x, up_y, down_y, low)
    up_d, down_d = flip(up_x, step_y), flip(down_y, step_x)
    own = [w_up, up_x, w_down, down_x]
    own_far = [flip(piece, core) for piece in own]
    other = [up_y, up_d, down_y, down_d]
    early_far = [flip(piece, core) for piece in other[::2]]
    *own_far, late_0, late_1 = together(*own_far, *early_far)
    early_far = [late_0, late_1]

    def arranged(near, far):
        pieces = near[:2] + far[:2] + near[2:] + far[2:]
        return [piece.reshape(-1, part_hidden) for piece in pieces]

    b_up = b_up.reshape(2, half, 1, part_hidden)
    anywhere = pl.BlockSpec(memory_space=pl.ANY)
    strips = [anywhere] * 8
    strip_outs = [(((width, part_hidden), BF16), anywhere)] * 4
    strip_outs += [(((2, 1, part_hidden), F32), whole((2, 1, part_hidden)))]
    copied = [
        pltpu.VMEM((2, 2, width, part_hidden), BF16),
        pltpu.VMEM((2, 2, width, part_hidden), BF16),
        pltpu.SemaphoreType.DMA((12,)),
        pltpu.SemaphoreType.DMA((4,)),
    ]
    cost = 6 * total_rows * width * hidden, 10 * weights
    *g_own, gb_own, sum_y, sum_h = call(
        functools.partial(feed_forward, False),
        (1,),
        [whole(full), whole(full[::-1])] * 2 + strips + [whole((2, 1, part_hidden))],
        strip_outs + [((full, F32), whole(full))] * 2,
        copied,
        *cost,
        low,
        low_t,
        top,
        top_t,
        *arranged(own, own_far),
        b_up[:, 0],
    )
    other[1], other[3], sum_y = together(other[1], other[3], sum_y)
    late_far = [flip(piece, core) for piece in other[1::2]]
    other_far = [early_far[0], late_far[0], early_far[1], late_far[1]]

    rest_bits = held[1:]
    shape = (2,) * len(rest_bits)
    tile = (part_rows, part_hidden)

    def pair(near, far, tile):
        near = near.reshape(shape[1:] + tile)
        return [near, flip(far.reshape(near.shape), core)]

    gup_own, gdown_own = pair(*g_own[:2], tile), pair(*g_own[2:], tile)
    *g_other, gb_other, layer_out, grad_middle, grad_attn, grad_context, sums_two = call(
        functools.partial(feed_forward, True),
        (1,),
        [whole(full), whole(full[::-1])] * 2
        + strips
        + [whole((2, 1, part_hidden)), smem, whole(vectors.shape)]
        + [anywhere] * 4,
        strip_outs
        + [
            ((full, BF16), whole(full)),
            ((full, F32), whole(full)),
            ((full, BF16), whole(full)),
            (((n_head,) + slab, BF16), whole((n_head,) + slab)),
            (((4, width), F32), whole((4, width))),
        ],
        [pltpu.VMEM(full, F32)] * 2
        + copied
        + [pltpu.VMEM(full, F32), pltpu.VMEM((width, width), BF16)]
        + [pltpu.VMEM(full, F32)] * 2,
        *cost,
        low,
        low_t,
        top,
        top_t,
        *arranged(other, other_far),
        b_up[:, 1],
        order_chunks,
        vectors,
        middle,
        w_out,
        sum_y,
        sum_h,
    )
    g_bu = jnp.stack([gb_own, gb_other], axis=1).reshape(n_head, 1, part_hidden)
    gup_other, gdown_other = pair(*g_other[:2], tile), pair(*g_other[2:], tile)

    def low_total(terms):
        return total(terms).astype(BF16)

    away = [
        low_total(side(gdown_own, 1, 0)),
        low_total(side(gup_other, 1, 0)),
        low_total(side(gdown_other, 1, 0)),
        low_total(side(gup_other, 0, 0)),
    ]
    down_01, up_11 = flip(away[0], step_x), flip(away[1], step_y)
    down_11, up_10 = flip(away[2], step_x), flip(away[3], step_y)
    grad_context, *_ = together(grad_context, *away)
    tokens_grad, gqk_near, gqk_far, gvo_near, gvo_far, g_b, sums_one = call(
        functools.partial(attention_backward, item_count),
        (n_head,),
        [whole(full), whole(vectors.shape)]
        + first_specs
        + [chunk(slab)] * 3
        + [chunk((pairs, padded, padded)), chunk(slab), whole(full)],
        [
            ((full, BF16), whole(full)),
            (((half,) + two_cols, BF16), near(two_cols)),
            (((half,) + two_cols, BF16), far(two_cols)),
            (((half,) + one_col, BF16), near(one_col)),
            (((half,) + one_col, BF16), far(one_col)),
            (((n_head, 1, 3 * part_cols), F32), chunk((1, 3 * part_cols))),
            (((2, width), F32), whole((2, width))),
        ],
        [
            pltpu.VMEM(full, F32),
            pltpu.VMEM((total_rows, 1), F32),
            pltpu.VMEM(full[::-1], BF16),
            pltpu.VMEM(full, F32),
        ],
        16 * total_rows * weights,
        12 * weights,
        x,
        vectors,
        near_qk,
        far_qk,
        near_vo,
        far_vo,
        query,
        key,
        value,
        probs,
        grad_context,
        grad_middle,
    )
    two = (part_rows, 2 * part_cols)
    down_01, up_11, down_11, up_10, gqk_near, gqk_far, gvo_near, gvo_far = together(
        down_01, up_11, down_11, up_10, gqk_near, gqk_far, gvo_near, gvo_far
    )

    def pair_first(near, far):
        return [near.reshape(shape + two), flip(far.reshape(shape + two), core)]

    away_up = low_total(side(gup_own, 1, 0) + [up_11])
    away_down = low_total(side(gdown_other, 0, 0) + [down_11])
    up_01, down_10 = flip(away_up, step_x), flip(away_down, step_y)
    qk_terms = pair_first(gqk_near, gqk_far)
    grad_attn, *_ = together(grad_attn, away_up, away_down, gqk_far)
    (g_out,) = call(
        out_gradient,
        (1,),
        [smem, whole((n_head,) + slab), whole(full), whole((width, width))],
        [(((width, width), BF16), whole((width, width)))],
        [],
        0,
        0,
        order_chunks,
        context,
        grad_attn,
        turn,
    )
    g_out = g_out.reshape(devices, -1, width)[ranks]
    g_out = g_out.reshape(devices, -1, n_head, part_cols).transpose(0, 2, 1, 3)
    g_out = g_out.reshape(n_head, width, part_cols)
    gvo_near = jnp.concatenate([gvo_near, g_out[:half]], axis=2)
    gvo_far = jnp.concatenate([gvo_far, g_out[half:]], axis=2)
    up_01, down_10, gvo_near, gvo_far, *qk_terms = together(
        up_01, down_10, gvo_near, gvo_far, *qk_terms
    )
    vo_terms = pair_first(gvo_near, gvo_far)
    have_qk, have_vo = list(rest_bits), list(rest_bits)
    up_terms = side(gup_own, 0, 0) + [up_10, up_01]
    down_terms = side(gdown_own, 0, 0) + [down_01, down_10]
    have_up = list(dp_bits[:-1][::-1])

    def descend(terms, steps, have):
        for step in steps:
            terms = shrink(terms, step, have)
        return terms

    def lockstep(*chains):
        flat = together(*(chain[-1] for chain in chains))
        return [chain[:-1] + [last] for chain, last in zip(chains, flat)]

    def descend_joined(one, other, axis, step, have):
        place = have.index(step)
        have.remove(step)
        away = [total(side(terms, 1, place)).astype(BF16) for terms in (one, other)]
        near = [total(side(terms, 0, place)) for terms in (one, other)]
        away = flip(jnp.concatenate(away, axis=axis), step)
        return [jnp.concatenate(near, axis=axis).astype(BF16), away]

    qk_terms = descend(qk_terms, along_y[:1], have_qk)
    vo_terms = descend(vo_terms, along_x, have_vo)
    back_z = along_z[::-1]
    rest_terms = descend_joined(up_terms, down_terms, -2, back_z[0], have_up)
    sums_shape = (devices, small_size)
    (sums,) = call(
        functools.partial(collect_vectors, per),
        (1,),
        [smem, whole(sums_one.shape), whole(sums_two.shape), whole(g_b.shape), whole(g_bu.shape)]
        + [whole((width, width))],
        [((sums_shape, F32), whole(sums_shape))],
        [],
        0,
        4 * width * width,
        order_chunks,
        sums_one,
        sums_two,
        g_b,
        g_bu,
        turn,
    )
    layer_out = turned_back(layer_out)
    rest_terms, qk_terms, vo_terms, swapped, (layer_out,) = lockstep(
        rest_terms, qk_terms, vo_terms, [exchange(sums)], [layer_out]
    )
    qk_terms = descend(qk_terms, along_y[1:] + along_x, have_qk)
    vo_terms = descend(vo_terms, along_y, have_vo)
    rest_terms = descend(rest_terms, back_z[1:], have_up)
    layer_out = unpad(layer_out)
    tokens_grad = unpad(turned_back(tokens_grad))

    rest_terms, qk_terms, vo_terms = lockstep(rest_terms, qk_terms, vo_terms)
    chains = [qk_terms, vo_terms]
    for step in back_z[:-2]:
        chains = [descend(terms, [step], list(have_qk)) for terms in chains]
        have_qk.remove(step)

    def corner(i, j):
        return jnp.concatenate(
            [total(side(side(terms, i, 0), j, 0)) for terms in chains], axis=-1
        )

    step, other = back_z[-2:]
    first = [
        corner(0, 0),
        flip(corner(1, 1).astype(BF16), both(step, other)),
        flip(corner(1, 0).astype(BF16), step),
        flip(corner(0, 1).astype(BF16), other),
    ]
    rest = total(rest_terms)
    g_up, g_down_t = rest[:part_rows], rest[part_rows:]
    first = total(first)
    g_qkv = first[:, : 3 * part_cols].reshape(part_rows, 3, part_cols)
    g_out = first[:, 3 * part_cols :].reshape(n_head, -1, part_cols).transpose(1, 0, 2)
    g_out = g_out.reshape(out_weight.shape)
    sums = jnp.sum(swapped[0], axis=0)

    def part(index):
        return sums[index * per : (index + 1) * per]

    return (
        layer_out,
        tokens_grad,
        part(0),
        part(1),
        g_qkv,
        sums[6 * per : 8 * per].reshape(2, per),
        g_out,
        part(2),
        part(3),
        part(4),
        g_up,
        sums[8 * per :],
        g_down_t.T,
        part(5),
    )


def solution(mesh):
    n_dp, n_head = mesh.shape["dp"], mesh.shape["head"]

    def run(*args):
        return local(n_dp, n_head, *args)

    return jax.shard_map(
        run,
        mesh=mesh,
        in_specs=(
            P(ALL, None),
            P("dp"),
            P(ALL),
            P(ALL),
            P("dp", None, "head"),
            P(None, ("head", "dp")),
            P(ALL, None),
            P(ALL),
            P(ALL),
            P(ALL),
            P("dp", "head"),
            P(("head", "dp")),
            P("head", "dp"),
            P(ALL),
            P(ALL, None),
        ),
        out_specs=(
            P(ALL, None),
            P(ALL, None),
            P(ALL),
            P(ALL),
            P("dp", None, "head"),
            P(None, ("head", "dp")),
            P(ALL, None),
            P(ALL),
            P(ALL),
            P(ALL),
            P("dp", "head"),
            P(("head", "dp")),
            P("head", "dp"),
            P(ALL),
        ),
        check_vma=False,
    )
```

profile of v0, /device:TPU:0, one launch (start us, length us, event | category | flops | bytes accessed | tf_op | source)
XLA Modules:
  0.0 258.8 jit_solution(926173496179370041)
XLA Ops:
  0.7 1.1 copy.54
  3.0 4.1 %collective-permute-start = (bf16[96,768]{1,0:T(8,128)(2,1)S(1)}, bf16[96,768]{1,0:T(8,128)(2,1)S(1)}, u32[]{:S(2)}, u32[]{:S(2)}) collective-permute-start(bf16[96,768]{1,0:T(8,128)(2,1)S(1)} %pad_maximum_fusion.13), channel_id=1, source_target_pairs={{0,16},{4,20},{8,24},{12,28},{16,0},{20,4},{24,8},{28,12},{1,17},{... | collective-permute-start | bytes 442376 | tf_op jit(solution)/shard_map/ppermute | solution.py:526
  7.1 1.6 collective-permute-start.1
  12.3 6.1 %all-to-all-start = ((bf16[32,2,144]{2,1,0:T(2,128)(2,1)}), bf16[32,2,144]{2,1,0:T(2,128)(2,1)S(1)}, u32[]{:S(2)}, u32[]{:S(2)}) async-start(bf16[32,2,144]{2,1,0:T(2,128)(2,1)} %reshape.721), calls=%async_computation | async-start | bytes 65536 | tf_op jit(solution)/shard_map/all_to_all | solution.py:571
  18.9 1.5 fusion.7.x
  20.5 1.6 fusion.8.top
  22.2 3.5 %all-to-all-done = bf16[32,2,144]{2,1,0:T(2,128)(2,1)S(1)} async-done(((bf16[32,2,144]{2,1,0:T(2,128)(2,1)}), bf16[32,2,144]{2,1,0:T(2,128)(2,1)S(1)}, u32[]{:S(2)}, u32[]{:S(2)}) %all-to-all-start) | async-done | bytes 18464 | tf_op jit(solution)/shard_map/all_to_all | solution.py:571
  27.8 1.5 fusion.3.turn
  30.8 2.5 shard_map.254
  33.3 2.4 collective-permute-done.4
  36.0 8.9 %collective-permute-done.5 = bf16[192,768]{1,0:T(8,128)(2,1)S(1)} collective-permute-done((bf16[192,768]{1,0:T(8,128)(2,1)S(1)}, bf16[192,768]{1,0:T(8,128)(2,1)S(1)}, u32[]{:S(2)}, u32[]{:S(2)}) %collective-permute-start.5) | collective-permute-done | bytes 294944 | tf_op jit(solution)/shard_map/ppermute | solution.py:526
  45.0 1.5 collective-permute-start.7
  46.4 1.1 collective-permute-start.6
  47.5 12.7 %collective-permute-done.7 = bf16[2,2,2,96,384]{4,3,2,1,0:T(8,128)(2,1)S(1)} collective-permute-done((bf16[2,2,2,96,384]{4,3,2,1,0:T(8,128)(2,1)S(1)}, bf16[2,2,2,96,384]{4,3,2,1,0:T(8,128)(2,1)S(1)}, u32[]{:S(2)}, u32[]{:S(2)}) %collective-permute-start.7) | collective-permute-done | bytes 589856 | tf_op jit(solution)/shard_map/ppermute | solution.py:526
  61.4 1.2 pad_maximum_fusion.5
  64.7 1.3 collective-permute-start.12
  66.8 1.3 collective-permute-start.9
  68.0 1.2 dynamic_slice.3.lengths
  70.2 1.9 copy.72
  72.2 3.1 %reshape.620 = bf16[32,24,768]{2,1,0:T(8,128)(2,1)S(1)} reshape(bf16[32,24,4,192]{3,2,1,0:T(4,128)(2,1)} %bitcast.283) | data formatting | bytes 2359296 | tf_op jit(solution)/shard_map/reshape | solution.py:709
  75.3 1.7 gather_fusion
  77.1 3.4 %fusion.6.w_out.rest_12_ = bf16[768,768]{1,0:T(8,128)(2,1)} fusion(bf16[768,768]{1,0:T(8,128)(2,1)} %bitcast.306, s32[768]{0:T(1024)S(1)} %fusion.43), kind=kOutput, calls=%fused_computation.12 | convolution fusion | flops 907149312 | bytes 2362368 | tf_op jit(solution)/shard_map/dot_general | solution.py:20
  80.5 10.3 %shard_map.255 = (bf16[4,384,192]{2,1,0:T(8,128)(2,1)}, bf16[4,384,192]{2,1,0:T(8,128)(2,1)}, bf16[4,384,192]{2,1,0:T(8,128)(2,1)}, f32[4,6,192,192]{3,2,1,0:T(8,128)}, bf16[4,384,192]{2,1,0:T(8,128)(2,1)}) custom-call(s32[2]{0:T(128)} %dynamic_slice.3.lengths, s32[4]{0:T(128)} %get-tuple-element.292.order.rest_9_, bf16[384,768]{1,0:T(8,128)(2,1)} %fusion.7.x, ...), custom_call_target="tpu_custom_call" | custom-call | flops 226492416 | bytes 884736 | tf_op jit(solution)/shard_map/pallas_call | solution.py:477
  90.8 5.1 %shard_map.256 = (f32[384,768]{1,0:T(8,128)}, bf16[384,768]{1,0:T(8,128)(2,1)}, bf16[768,384]{1,0:T(8,128)(2,1)}, bf16[768,384]{1,0:T(8,128)(2,1)}) custom-call(s32[4]{0:T(128)} %get-tuple-element.292.order.rest_9_, bf16[384,768]{1,0:T(8,128)(2,1)} %fusion.7.x, bf16[4,384,192]{2,1,0:T(8,128)(2,1)} %get-tuple-element.119.ctx, ...), custom_call_target="tpu_custom_call" | custom-call | flops 56623104 | bytes 589824 | tf_op jit(solution)/shard_map/pallas_call | solution.py:477
  98.2 1.1 collective-permute-start.24
  101.7 11.9 %shard_map.257 = (bf16[768,768]{1,0:T(8,128)(2,1)}, bf16[768,768]{1,0:T(8,128)(2,1)}, bf16[768,768]{1,0:T(8,128)(2,1)}, bf16[768,768]{1,0:T(8,128)(2,1)}, f32[2,...) custom-call(bf16[384,768]{1,0:T(8,128)(2,1)} %get-tuple-element.122.hidden, ...), custom_call_target="tpu_custom_call" | custom-call | flops 679477248 | bytes 737280 | tf_op jit(solution)/shard_map/pallas_call | solution.py:477
  115.4 1.7 collective-permute-done.26
  118.8 14.5 %shard_map.258 = (bf16[768,768]{1,0:T(8,128)(2,1)}, bf16[768,768]{1,0:T(8,128)(2,1)}, bf16[768,768]{1,0:T(8,128)(2,1)}, bf16[768,768]{1,0:T(8,128)(2,1)}, f32[2,...) custom-call(bf16[384,768]{1,0:T(8,128)(2,1)} %get-tuple-element.122., ...), custom_call_target="tpu_custom_call" | custom-call | flops 679477248 | bytes 737280 | tf_op jit(solution)/shard_map/pallas_call | solution.py:477
  134.7 1.2 copy-done.13
  138.1 1.1 collective-permute-start.31
  139.2 1.4 fusion.15
  140.5 1.1 collective-permute-start.29
  143.4 21.0 %shard_map.259 = (bf16[384,768]{1,0:T(8,128)(2,1)}, bf16[2,768,384]{2,1,0:T(8,128)(2,1)}, bf16[2,768,384]{2,1,0:T(8,128)(2,1)}, bf16[2,768,192]{2,1,0:T(8,128)(2...) custom-call(bf16[384,768]{1,0:T(8,128)(2,1)} %fusion.7.x, ...), custom_call_target="tpu_custom_call" | custom-call | flops 452984832 | bytes 884736 | tf_op jit(solution)/shard_map/pallas_call | solution.py:477
  164.4 3.9 %collective-permute-done.32 = bf16[2,2,96,768]{3,2,1,0:T(8,128)(2,1)} collective-permute-done((bf16[2,2,96,768]{3,2,1,0:T(8,128)(2,1)}, bf16[2,2,96,768]{3,2,1,0:T(8,128)(2,1)}, u32[]{:S(2)}, u32[]{:S(2)}) %collective-permute-start.32) | collective-permute-done | bytes 589856 | tf_op jit(solution)/shard_map/ppermute | solution.py:526
  168.3 2.1 fusion.12
  170.4 1.1 collective-permute-start.34
  171.5 2.3 fusion.14
  174.8 5.8 %shard_map.260 = bf16[768,768]{1,0:T(8,128)(2,1)} custom-call(s32[4]{0:T(128)} %get-tuple-element.292.order.rest_9_, bf16[4,384,192]{2,1,0:T(8,128)(2,1)} %get-tuple-element.119.ctx, bf16[384,768]{1,0:T(8,128)(2,1)} %get-tuple-element.167.grad_attn, bf16[768,768]{1,0:T(8,128)(2,1)} %fusion.3.turn), custom_call_target="tpu_custom_call" | custom-call | tf_op jit(solution)/shard_map/pallas_call | solution.py:477
  180.6 2.0 gather_fusion.1
  182.6 1.4 reshape.644
  187.1 2.5 collective-permute-done.33
  189.7 2.0 fusion.24
  192.6 1.8 fusion.30
  194.4 1.5 fusion.29
  200.3 2.9 %shard_map.261 = f32[32,288]{1,0:T(8,128)} custom-call(s32[4]{0:T(128)} %get-tuple-element.292.order.rest_9_, f32[2,768]{1,0:T(2,128)} %get-tuple-element.177.sums_one, f32[4,768]{1,0:T(4,128)} %get-tuple-element.178.sums_two, f32[4,1,576]{2,1,0:T(1,128)} %get-tuple-element.179.g_b, f32[4,1,768]{2,1,0:T(1,128)} %reshape.649.g_bu, bf16[768,768]{1,0:T(8,128)(2,1)} %fusion.3.turn), custom_call_target="tpu_custom_call" | custom-call | bytes 294912 | tf_op jit(solution)/shard_map/pallas_call | solution.py:477
  203.2 1.5 copy.60
  204.7 3.5 %all-to-all-start.1 = ((f32[32,1,288]{2,1,0:T(1,128)}), f32[32,1,288]{2,1,0:T(1,128)}, u32[]{:S(2)}, u32[]{:S(2)}) async-start(f32[32,1,288]{2,1,0:T(1,128)} %copy.60), calls=%async_computation.1 | async-start | bytes 98304 | tf_op jit(solution)/shard_map/all_to_all | solution.py:571
  208.2 1.5 fusion.9
  209.8 5.5 %all-to-all-done.1 = f32[32,1,288]{2,1,0:T(1,128)} async-done(((f32[32,1,288]{2,1,0:T(1,128)}), f32[32,1,288]{2,1,0:T(1,128)}, u32[]{:S(2)}, u32[]{:S(2)}) %all-to-all-start.1) | async-done | bytes 36896 | tf_op jit(solution)/shard_map/all_to_all | solution.py:571
  215.3 1.4 copy.73
  216.7 1.9 fusion.27
  219.2 1.9 fusion.28
  222.0 1.7 fusion.33
  223.8 1.7 collective-permute-start.40
  225.4 1.5 fusion.10
  226.9 2.1 reshape.653
  232.6 7.1 %collective-permute-done.40 = bf16[192,768]{1,0:T(8,128)(2,1)} collective-permute-done((bf16[192,768]{1,0:T(8,128)(2,1)}, bf16[192,768]{1,0:T(8,128)(2,1)}, u32[]{:S(2)}, u32[]{:S(2)}) %collective-permute-start.40) | collective-permute-done | bytes 294944 | tf_op jit(solution)/shard_map/ppermute | solution.py:526
  239.8 1.1 bitcast_add_fusion
  240.9 1.4 fusion.42
  242.3 1.4 fusion.41
  243.7 1.7 collective-permute-start.43
  245.6 2.8 %collective-permute-start.45 = (bf16[96,768]{1,0:T(8,128)(2,1)S(1)}, bf16[96,768]{1,0:T(8,128)(2,1)S(1)}, u32[]{:S(2)}, u32[]{:S(2)}) collective-permute-start(bf16[96,768]{1,0:T(8,128)(2,1)S(1)} %pad_maximum_fusion.16), channel_id=1, source_target_pairs={{0,16},{4,20},{8,24},{12,28},{16,0},{20,4},{24,8},{28,12},{1,17},{... | collective-permute-start | bytes 442376 | tf_op jit(solution)/shard_map/ppermute | solution.py:526
  249.2 3.1 %collective-permute-done.43 = bf16[96,768]{1,0:T(8,128)(2,1)S(1)} collective-permute-done((bf16[96,768]{1,0:T(8,128)(2,1)S(1)}, bf16[96,768]{1,0:T(8,128)(2,1)S(1)}, u32[]{:S(2)}, u32[]{:S(2)}) %collective-permute-start.43) | collective-permute-done | bytes 147488 | tf_op jit(solution)/shard_map/ppermute | solution.py:526
  252.3 4.0 %collective-permute-done.44 = bf16[96,768]{1,0:T(8,128)(2,1)S(1)} collective-permute-done((bf16[96,768]{1,0:T(8,128)(2,1)S(1)}, bf16[96,768]{1,0:T(8,128)(2,1)S(1)}, u32[]{:S(2)}, u32[]{:S(2)}) %collective-permute-start.44) | collective-permute-done | bytes 147488 | tf_op jit(solution)/shard_map/ppermute | solution.py:526
  (224 shorter events, 45.6 us)
Async XLA Ops:
  0.6 17.9 %copy-start.25 = (bf16[370,768]{1,0:T(8,128)(2,1)S(1)}, bf16[370,768]{1,0:T(8,128)(2,1)}, u32[]{:S(2)}) copy-start(bf16[370,768]{1,0:T(8,128)(2,1)} %param.15) | copy-start | bytes 1704964
  1.8 16.9 %copy-start.26 = (bf16[370,768]{1,0:T(8,128)(2,1)S(1)}, bf16[370,768]{1,0:T(8,128)(2,1)}, u32[]{:S(2)}) copy-start(bf16[370,768]{1,0:T(8,128)(2,1)} %param.29) | copy-start | bytes 1704964
  3.0 23.4 %collective-permute-start = (bf16[96,768]{1,0:T(8,128)(2,1)S(1)}, bf16[96,768]{1,0:T(8,128)(2,1)S(1)}, u32[]{:S(2)}, u32[]{:S(2)}) collective-permute-start(bf16[96,768]{1,0:T(8,128)(2,1)S(1)} %pad_maximum_fusion.13), channel_id=1, source_target_pairs={{0,16},{4,20},{8,24},{12,28},{16,0},{20,4},{24,8},{28,12},{1,17},{... | collective-permute-start | bytes 442376 | tf_op jit(solution)/shard_map/ppermute | solution.py:526
  7.1 19.2 %collective-permute-start.1 = (bf16[96,768]{1,0:T(8,128)(2,1)S(1)}, bf16[96,768]{1,0:T(8,128)(2,1)S(1)}, u32[]{:S(2)}, u32[]{:S(2)}) collective-permute-start(bf16[96,768]{1,0:T(8,128)(2,1)S(1)} %pad_maximum_fusion.13), channel_id=1, source_target_pairs={{0,8},{4,12},{8,0},{12,4},{16,24},{20,28},{24,16},{28,20},{1,9},{5... | collective-permute-start | bytes 442376 | tf_op jit(solution)/shard_map/ppermute | solution.py:526
  8.7 17.7 %collective-permute-start.2 = (bf16[96,768]{1,0:T(8,128)(2,1)S(1)}, bf16[96,768]{1,0:T(8,128)(2,1)S(1)}, u32[]{:S(2)}, u32[]{:S(2)}) collective-permute-start(bf16[96,768]{1,0:T(8,128)(2,1)S(1)} %pad_maximum_fusion.13), channel_id=1, source_target_pairs={{0,24},{4,28},{8,16},{12,20},{16,8},{20,12},{24,0},{28,4},{1,25},{... | collective-permute-start | bytes 442376 | tf_op jit(solution)/shard_map/ppermute | solution.py:526
  12.3 13.3 %all-to-all-start = ((bf16[32,2,144]{2,1,0:T(2,128)(2,1)}), bf16[32,2,144]{2,1,0:T(2,128)(2,1)S(1)}, u32[]{:S(2)}, u32[]{:S(2)}) async-start(bf16[32,2,144]{2,1,0:T(2,128)(2,1)} %reshape.721), calls=%async_computation | async-start | bytes 65536 | tf_op jit(solution)/shard_map/all_to_all | solution.py:571
  18.5 58.5 %copy-start.30 = (s32[768]{0:T(1024)}, s32[768]{0:T(1024)S(1)}, u32[]{:S(2)}) copy-start(s32[768]{0:T(1024)S(1)} %fusion.43) | copy-start | bytes 9220
  26.6 9.1 %collective-permute-start.4 = (bf16[2,2,96,384]{3,2,1,0:T(8,128)(2,1)S(1)}, bf16[2,2,96,384]{3,2,1,0:T(8,128)(2,1)S(1)}, u32[]{:S(2)}, u32[]{:S(2)}) collective-permute-start(bf16[2,2,96,384]{3,2,1,0:T(8,128)(2,1)S(1)} %get-tuple-element.278), channel_id=1, source_target_pairs={{0,2},{1,3},{2,0},{3,1},{4,6},{5,7},{6,4},{7,5},{8,10},{9,11},{10,... | collective-permute-start | bytes 884744 | tf_op jit(solution)/shard_map/ppermute | solution.py:526
  27.1 8.7 %collective-permute-start.3 = (bf16[2,2,96,384]{3,2,1,0:T(8,128)(2,1)S(1)}, bf16[2,2,96,384]{3,2,1,0:T(8,128)(2,1)S(1)}, u32[]{:S(2)}, u32[]{:S(2)}) collective-permute-start(bf16[2,2,96,384]{3,2,1,0:T(8,128)(2,1)S(1)} %get-tuple-element.279), channel_id=1, source_target_pairs={{0,4},{4,0},{8,12},{12,8},{16,20},{20,16},{24,28},{28,24},{1,5},{5... | collective-permute-start | bytes 884744 | tf_op jit(solution)/shard_map/ppermute | solution.py:526
  29.3 15.6 %collective-permute-start.5 = (bf16[192,768]{1,0:T(8,128)(2,1)S(1)}, bf16[192,768]{1,0:T(8,128)(2,1)S(1)}, u32[]{:S(2)}, u32[]{:S(2)}) collective-permute-start(bf16[192,768]{1,0:T(8,128)(2,1)S(1)} %pad_maximum_fusion.12), channel_id=1, source_target_pairs={{0,16},{4,20},{8,24},{12,28},{16,0},{20,4},{24,8},{28,12},{1,17},{... | collective-permute-start | bytes 884744 | tf_op jit(solution)/shard_map/ppermute | solution.py:526
  45.0 15.3 %collective-permute-start.7 = (bf16[2,2,2,96,384]{4,3,2,1,0:T(8,128)(2,1)S(1)}, bf16[2,2,2,96,384]{4,3,2,1,0:T(8,128)(2,1)S(1)}, u32[]{:S(2)}, u32[]{:S(2)}) collective-permute-start(bf16[2,2,2,96,384]{4,3,2,1,0:T(8,128)(2,1)S(1)} %pad_maximum_fusion.8), channel_id=1, source_target_pairs={{0,4},{4,0},{8,12},{12,8},{16,20},{20,16},{24,28},{28,24},{1,5},{5... | collective-permute-start | bytes 1769480 | tf_op jit(solution)/shard_map/ppermute | solution.py:526
  46.4 14.9 %collective-permute-start.8 = (bf16[2,192,768]{2,1,0:T(8,128)(2,1)S(1)}, bf16[2,192,768]{2,1,0:T(8,128)(2,1)S(1)}, u32[]{:S(2)}, u32[]{:S(2)}) collective-permute-start(bf16[2,192,768]{2,1,0:T(8,128)(2,1)S(1)} %pad_maximum_fusion.9), channel_id=1, source_target_pairs={{0,8},{4,12},{8,0},{12,4},{16,24},{20,28},{24,16},{28,20},{1,9},{5... | collective-permute-start | bytes 1769480 | tf_op jit(solution)/shard_map/ppermute | solution.py:526
  46.4 16.1 %collective-permute-start.6 = (bf16[2,2,2,96,384]{4,3,2,1,0:T(8,128)(2,1)S(1)}, bf16[2,2,2,96,384]{4,3,2,1,0:T(8,128)(2,1)S(1)}, u32[]{:S(2)}, u32[]{:S(2)}) collective-permute-start(bf16[2,2,2,96,384]{4,3,2,1,0:T(8,128)(2,1)S(1)} %pad_maximum_fusion.7), channel_id=1, source_target_pairs={{0,2},{1,3},{2,0},{3,1},{4,6},{5,7},{6,4},{7,5},{8,10},{9,11},{10,... | collective-permute-start | bytes 1769480 | tf_op jit(solution)/shard_map/ppermute | solution.py:526
  60.5 8.8 %copy-start = (bf16[2,2,2,2,96,384]{5,4,3,2,1,0:T(8,128)(2,1)}, bf16[2,2,2,2,96,384]{5,4,3,2,1,0:T(8,128)(2,1)S(1)}, u32[]{:S(2)}) copy-start(bf16[2,2,2,2,96,384]{5,4,3,2,1,0:T(8,128)(2,1)S(1)} %copy.57) | copy-start | bytes 3538948
  62.7 7.2 %copy-start.1 = (bf16[2,768,384]{2,1,0:T(8,128)(2,1)}, bf16[2,768,384]{2,1,0:T(8,128)(2,1)S(1)}, u32[]{:S(2)}) copy-start(bf16[2,768,384]{2,1,0:T(8,128)(2,1)S(1)} %pad_maximum_fusion.1.qk_near) | copy-start | bytes 3538948
  62.7 4.0 %collective-permute-start.14 = (bf16[2,768,384]{2,1,0:T(8,128)(2,1)S(1)}, bf16[2,768,384]{2,1,0:T(8,128)(2,1)S(1)}, u32[]{:S(2)}, u32[]{:S(2)}) collective-permute-start(bf16[2,768,384]{2,1,0:T(8,128)(2,1)S(1)} %bitcast.277), channel_id=1, source_target_pairs={{0,1},{1,0},{2,3},{3,2},{4,5},{5,4},{6,7},{7,6},{8,9},{9,8},{10,11... | collective-permute-start | bytes 3538952 | tf_op jit(solution)/shard_map/ppermute | solution.py:526
  62.8 14.3 %collective-permute-start.13 = (bf16[2,768,384]{2,1,0:T(8,128)(2,1)S(1)}, bf16[2,768,384]{2,1,0:T(8,128)(2,1)}, u32[]{:S(2)}, u32[]{:S(2)}) collective-permute-start(bf16[2,768,384]{2,1,0:T(8,128)(2,1)S(1)} %pad_maximum_fusion.1.qk_near), channel_id=1, source_target_pairs={{0,1},{1,0},{2,3},{3,2},{4,5},{5,4},{6,7},{7,6},{8,9},{9,8},{10,11... | collective-permute-start | bytes 3538952 | tf_op jit(solution)/shard_map/ppermute | solution.py:526
  63.9 32.0 %collective-permute-start.10 = (bf16[2,2,96,768]{3,2,1,0:T(8,128)(2,1)}, bf16[2,2,96,768]{3,2,1,0:T(8,128)(2,1)}, u32[]{:S(2)}, u32[]{:S(2)}) collective-permute-start(bf16[2,2,96,768]{3,2,1,0:T(8,128)(2,1)} %get-tuple-element.113), channel_id=1, source_target_pairs={{0,4},{4,0},{8,12},{12,8},{16,20},{20,16},{24,28},{28,24},{1,5},{5... | collective-permute-start | bytes 1769480 | tf_op jit(solution)/shard_map/ppermute | solution.py:526
  64.7 31.8 %collective-permute-start.12 = (bf16[2,2,96,768]{3,2,1,0:T(8,128)(2,1)}, bf16[2,2,96,768]{3,2,1,0:T(8,128)(2,1)}, u32[]{:S(2)}, u32[]{:S(2)}) collective-permute-start(bf16[2,2,96,768]{3,2,1,0:T(8,128)(2,1)} %get-tuple-element.113), channel_id=1, source_target_pairs={{0,2},{1,3},{2,0},{3,1},{4,6},{5,7},{6,4},{7,5},{8,10},{9,11},{10,... | collective-permute-start | bytes 1769480 | tf_op jit(solution)/shard_map/ppermute | solution.py:526
  66.0 30.5 %collective-permute-start.11 = (bf16[2,2,96,768]{3,2,1,0:T(8,128)(2,1)}, bf16[2,2,96,768]{3,2,1,0:T(8,128)(2,1)}, u32[]{:S(2)}, u32[]{:S(2)}) collective-permute-start(bf16[2,2,96,768]{3,2,1,0:T(8,128)(2,1)} %get-tuple-element.112), channel_id=1, source_target_pairs={{0,2},{1,3},{2,0},{3,1},{4,6},{5,7},{6,4},{7,5},{8,10},{9,11},{10,... | collective-permute-start | bytes 1769480 | tf_op jit(solution)/shard_map/ppermute | solution.py:526
  66.8 29.8 %collective-permute-start.9 = (bf16[2,2,96,768]{3,2,1,0:T(8,128)(2,1)}, bf16[2,2,96,768]{3,2,1,0:T(8,128)(2,1)}, u32[]{:S(2)}, u32[]{:S(2)}) collective-permute-start(bf16[2,2,96,768]{3,2,1,0:T(8,128)(2,1)} %get-tuple-element.112), channel_id=1, source_target_pairs={{0,4},{4,0},{8,12},{12,8},{16,20},{20,16},{24,28},{28,24},{1,5},{5... | collective-permute-start | bytes 1769480 | tf_op jit(solution)/shard_map/ppermute | solution.py:526
  77.1 20.1 %collective-permute-start.15 = (bf16[2,2,96,768]{3,2,1,0:T(8,128)(2,1)S(1)}, bf16[2,2,96,768]{3,2,1,0:T(8,128)(2,1)S(1)}, u32[]{:S(2)}, u32[]{:S(2)}) collective-permute-start(bf16[2,2,96,768]{3,2,1,0:T(8,128)(2,1)S(1)} %copy-done.4), channel_id=1, source_target_pairs={{0,1},{1,0},{2,3},{3,2},{4,5},{5,4},{6,7},{7,6},{8,9},{9,8},{10,11... | collective-permute-start | bytes 1769480 | tf_op jit(solution)/shard_map/ppermute | solution.py:526
  90.8 5.1 %copy-start.3 = (bf16[2,2,96,768]{3,2,1,0:T(8,128)(2,1)S(1)}, bf16[2,2,96,768]{3,2,1,0:T(8,128)(2,1)}, u32[]{:S(2)}) copy-start(bf16[2,2,96,768]{3,2,1,0:T(8,128)(2,1)} %get-tuple-element.113) | copy-start | bytes 1769476
  90.8 9.4 %copy-start.32 = (f32[4,1,768]{2,1,0:T(1,128)S(1)}, f32[4,1,768]{2,1,0:T(1,128)}, u32[]{:S(2)}) copy-start(f32[4,1,768]{2,1,0:T(1,128)} %get-tuple-element.133) | copy-start | bytes 36868
  96.0 2.2 collective-permute-start.17
  96.5 2.7 %collective-permute-start.16 = (bf16[2,2,96,768]{3,2,1,0:T(8,128)(2,1)}, bf16[2,2,96,768]{3,2,1,0:T(8,128)(2,1)S(1)}, u32[]{:S(2)}, u32[]{:S(2)}) collective-permute-start(bf16[2,2,96,768]{3,2,1,0:T(8,128)(2,1)} %collective-permute-done.9), channel_id=1, source_target_pairs={{0,1},{1,0},{2,3},{3,2},{4,5},{5,4},{6,7},{7,6},{8,9},{9,8},{10,11... | collective-permute-start | bytes 1769480 | tf_op jit(solution)/shard_map/ppermute | solution.py:526
  96.6 4.3 %collective-permute-start.18 = (bf16[2,2,96,768]{3,2,1,0:T(8,128)(2,1)}, bf16[2,2,96,768]{3,2,1,0:T(8,128)(2,1)S(1)}, u32[]{:S(2)}, u32[]{:S(2)}) collective-permute-start(bf16[2,2,96,768]{3,2,1,0:T(8,128)(2,1)} %collective-permute-done.10), channel_id=1, source_target_pairs={{0,1},{1,0},{2,3},{3,2},{4,5},{5,4},{6,7},{7,6},{8,9},{9,8},{10,11... | collective-permute-start | bytes 1769480 | tf_op jit(solution)/shard_map/ppermute | solution.py:526
  97.1 3.8 %collective-permute-start.19 = (bf16[2,2,96,768]{3,2,1,0:T(8,128)(2,1)}, bf16[2,2,96,768]{3,2,1,0:T(8,128)(2,1)}, u32[]{:S(2)}, u32[]{:S(2)}) collective-permute-start(bf16[2,2,96,768]{3,2,1,0:T(8,128)(2,1)} %collective-permute-done.11), channel_id=1, source_target_pairs={{0,1},{1,0},{2,3},{3,2},{4,5},{5,4},{6,7},{7,6},{8,9},{9,8},{10,11... | collective-permute-start | bytes 1769480 | tf_op jit(solution)/shard_map/ppermute | solution.py:526
  97.2 4.3 %copy-start.17 = (bf16[2,2,96,768]{3,2,1,0:T(8,128)(2,1)}, bf16[2,2,96,768]{3,2,1,0:T(8,128)(2,1)S(1)}, u32[]{:S(2)}) copy-start(bf16[2,2,96,768]{3,2,1,0:T(8,128)(2,1)S(1)} %collective-permute-done.15) | copy-start | bytes 1769476
  97.2 4.3 %collective-permute-start.20 = (bf16[2,2,96,768]{3,2,1,0:T(8,128)(2,1)}, bf16[2,2,96,768]{3,2,1,0:T(8,128)(2,1)S(1)}, u32[]{:S(2)}, u32[]{:S(2)}) collective-permute-start(bf16[2,2,96,768]{3,2,1,0:T(8,128)(2,1)} %collective-permute-done.12), channel_id=1, source_target_pairs={{0,1},{1,0},{2,3},{3,2},{4,5},{5,4},{6,7},{7,6},{8,9},{9,8},{10,11... | collective-permute-start | bytes 1769480 | tf_op jit(solution)/shard_map/ppermute | solution.py:526
  98.2 15.9 %collective-permute-start.24 = (bf16[2,2,96,768]{3,2,1,0:T(8,128)(2,1)}, bf16[2,2,96,768]{3,2,1,0:T(8,128)(2,1)}, u32[]{:S(2)}, u32[]{:S(2)}) collective-permute-start(bf16[2,2,96,768]{3,2,1,0:T(8,128)(2,1)} %collective-permute-done.9), channel_id=1, source_target_pairs={{0,2},{1,3},{2,0},{3,1},{4,6},{5,7},{6,4},{7,5},{8,10},{9,11},{10,... | collective-permute-start | bytes 1769480 | tf_op jit(solution)/shard_map/ppermute | solution.py:526
  99.3 15.6 %collective-permute-start.25 = (bf16[2,2,96,768]{3,2,1,0:T(8,128)(2,1)}, bf16[2,2,96,768]{3,2,1,0:T(8,128)(2,1)}, u32[]{:S(2)}, u32[]{:S(2)}) collective-permute-start(bf16[2,2,96,768]{3,2,1,0:T(8,128)(2,1)} %collective-permute-done.12), channel_id=1, source_target_pairs={{0,4},{4,0},{8,12},{12,8},{16,20},{20,16},{24,28},{28,24},{1,5},{5... | collective-permute-start | bytes 1769480 | tf_op jit(solution)/shard_map/ppermute | solution.py:526
  101.5 12.1 %copy-start.22 = (bf16[2,2,96,768]{3,2,1,0:T(8,128)(2,1)}, bf16[2,2,96,768]{3,2,1,0:T(8,128)(2,1)S(1)}, u32[]{:S(2)}) copy-start(bf16[2,2,96,768]{3,2,1,0:T(8,128)(2,1)S(1)} %collective-permute-done.20) | copy-start | bytes 1769476
  114.9 2.2 collective-permute-start.26
  114.9 3.1 %collective-permute-start.27 = (bf16[2,2,96,768]{3,2,1,0:T(8,128)(2,1)}, bf16[2,2,96,768]{3,2,1,0:T(8,128)(2,1)S(1)}, u32[]{:S(2)}, u32[]{:S(2)}) collective-permute-start(bf16[2,2,96,768]{3,2,1,0:T(8,128)(2,1)} %collective-permute-done.25), channel_id=1, source_target_pairs={{0,1},{1,0},{2,3},{3,2},{4,5},{5,4},{6,7},{7,6},{8,9},{9,8},{10,11... | collective-permute-start | bytes 1769480 | tf_op jit(solution)/shard_map/ppermute | solution.py:526
  115.4 20.5 %collective-permute-start.22 = (bf16[2,2,2,96,768]{4,3,2,1,0:T(8,128)(2,1)}, bf16[2,2,2,96,768]{4,3,2,1,0:T(8,128)(2,1)S(1)}, u32[]{:S(2)}, u32[]{:S(2)}) collective-permute-start(bf16[2,2,2,96,768]{4,3,2,1,0:T(8,128)(2,1)} %bitcast.345), channel_id=1, source_target_pairs={{0,1},{1,0},{2,3},{3,2},{4,5},{5,4},{6,7},{7,6},{8,9},{9,8},{10,11... | collective-permute-start | bytes 3538952 | tf_op jit(solution)/shard_map/ppermute | solution.py:526
  118.8 15.1 %copy-start.5 = (bf16[768,768]{1,0:T(8,128)(2,1)S(1)}, bf16[768,768]{1,0:T(8,128)(2,1)}, u32[]{:S(2)}) copy-start(bf16[768,768]{1,0:T(8,128)(2,1)} %get-tuple-element.136) | copy-start | bytes 3538948
  133.3 3.8 %collective-permute-start.30 = (bf16[2,2,2,96,768]{4,3,2,1,0:T(8,128)(2,1)}, bf16[2,2,2,96,768]{4,3,2,1,0:T(8,128)(2,1)S(1)}, u32[]{:S(2)}, u32[]{:S(2)}) collective-permute-start(bf16[2,2,2,96,768]{4,3,2,1,0:T(8,128)(2,1)} %bitcast.347), channel_id=1, source_target_pairs={{0,1},{1,0},{2,3},{3,2},{4,5},{5,4},{6,7},{7,6},{8,9},{9,8},{10,11... | collective-permute-start | bytes 3538952 | tf_op jit(solution)/shard_map/ppermute | solution.py:526
  133.5 5.6 %collective-permute-start.28 = (bf16[2,2,2,96,768]{4,3,2,1,0:T(8,128)(2,1)}, bf16[2,2,2,96,768]{4,3,2,1,0:T(8,128)(2,1)S(1)}, u32[]{:S(2)}, u32[]{:S(2)}) collective-permute-start(bf16[2,2,2,96,768]{4,3,2,1,0:T(8,128)(2,1)} %bitcast.346), channel_id=1, source_target_pairs={{0,1},{1,0},{2,3},{3,2},{4,5},{5,4},{6,7},{7,6},{8,9},{9,8},{10,11... | collective-permute-start | bytes 3538952 | tf_op jit(solution)/shard_map/ppermute | solution.py:526
  134.0 37.6 %collective-permute-start.21 = (bf16[2,2,2,96,768]{4,3,2,1,0:T(8,128)(2,1)}, bf16[2,2,2,96,768]{4,3,2,1,0:T(8,128)(2,1)}, u32[]{:S(2)}, u32[]{:S(2)}) collective-permute-start(bf16[2,2,2,96,768]{4,3,2,1,0:T(8,128)(2,1)} %bitcast.343), channel_id=1, source_target_pairs={{0,1},{1,0},{2,3},{3,2},{4,5},{5,4},{6,7},{7,6},{8,9},{9,8},{10,11... | collective-permute-start | bytes 3538952 | tf_op jit(solution)/shard_map/ppermute | solution.py:526
  136.1 28.2 %collective-permute-start.23 = (bf16[2,2,96,768]{3,2,1,0:T(8,128)(2,1)S(1)}, bf16[2,2,96,768]{3,2,1,0:T(8,128)(2,1)}, u32[]{:S(2)}, u32[]{:S(2)}) collective-permute-start(bf16[2,2,96,768]{3,2,1,0:T(8,128)(2,1)S(1)} %fusion.18), channel_id=1, source_target_pairs={{0,4},{4,0},{8,12},{12,8},{16,20},{20,16},{24,28},{28,24},{1,5},{5... | collective-permute-start | bytes 1769480 | tf_op jit(solution)/shard_map/ppermute | solution.py:526
  138.1 26.3 %collective-permute-start.31 = (bf16[2,2,96,768]{3,2,1,0:T(8,128)(2,1)}, bf16[2,2,96,768]{3,2,1,0:T(8,128)(2,1)}, u32[]{:S(2)}, u32[]{:S(2)}) collective-permute-start(bf16[2,2,96,768]{3,2,1,0:T(8,128)(2,1)} %fusion.16), channel_id=1, source_target_pairs={{0,4},{4,0},{8,12},{12,8},{16,20},{20,16},{24,28},{28,24},{1,5},{5... | collective-permute-start | bytes 1769480 | tf_op jit(solution)/shard_map/ppermute | solution.py:526
  139.2 4.2 %copy-start.11 = (bf16[768,768]{1,0:T(8,128)(2,1)S(1)}, bf16[768,768]{1,0:T(8,128)(2,1)}, u32[]{:S(2)}) copy-start(bf16[768,768]{1,0:T(8,128)(2,1)} %get-tuple-element.134) | copy-start | bytes 3538948
  140.5 23.8 %collective-permute-start.29 = (bf16[2,2,96,768]{3,2,1,0:T(8,128)(2,1)}, bf16[2,2,96,768]{3,2,1,0:T(8,128)(2,1)}, u32[]{:S(2)}, u32[]{:S(2)}) collective-permute-start(bf16[2,2,96,768]{3,2,1,0:T(8,128)(2,1)} %get-tuple-element.269), channel_id=1, source_target_pairs={{0,2},{1,3},{2,0},{3,1},{4,6},{5,7},{6,4},{7,5},{8,10},{9,11},{10,... | collective-permute-start | bytes 1769480 | tf_op jit(solution)/shard_map/ppermute | solution.py:526
  141.7 26.6 %collective-permute-start.32 = (bf16[2,2,96,768]{3,2,1,0:T(8,128)(2,1)}, bf16[2,2,96,768]{3,2,1,0:T(8,128)(2,1)}, u32[]{:S(2)}, u32[]{:S(2)}) collective-permute-start(bf16[2,2,96,768]{3,2,1,0:T(8,128)(2,1)} %get-tuple-element.268), channel_id=1, source_target_pairs={{0,2},{1,3},{2,0},{3,1},{4,6},{5,7},{6,4},{7,5},{8,10},{9,11},{10,... | collective-permute-start | bytes 1769480 | tf_op jit(solution)/shard_map/ppermute | solution.py:526
  168.3 21.3 %collective-permute-start.35 = (bf16[2,2,2,2,96,384]{5,4,3,2,1,0:T(8,128)(2,1)}, bf16[2,2,2,2,96,384]{5,4,3,2,1,0:T(8,128)(2,1)}, u32[]{:S(2)}, u32[]{:S(2)}) collective-permute-start(bf16[2,2,2,2,96,384]{5,4,3,2,1,0:T(8,128)(2,1)} %bitcast.344), channel_id=1, source_target_pairs={{0,1},{1,0},{2,3},{3,2},{4,5},{5,4},{6,7},{7,6},{8,9},{9,8},{10,11... | collective-permute-start | bytes 3538952 | tf_op jit(solution)/shard_map/ppermute | solution.py:526
  170.4 16.7 %collective-permute-start.34 = (bf16[2,2,96,768]{3,2,1,0:T(8,128)(2,1)}, bf16[2,2,96,768]{3,2,1,0:T(8,128)(2,1)}, u32[]{:S(2)}, u32[]{:S(2)}) collective-permute-start(bf16[2,2,96,768]{3,2,1,0:T(8,128)(2,1)} %fusion.12), channel_id=1, source_target_pairs={{0,2},{1,3},{2,0},{3,1},{4,6},{5,7},{6,4},{7,5},{8,10},{9,11},{10,... | collective-permute-start | bytes 1769480 | tf_op jit(solution)/shard_map/ppermute | solution.py:526
  173.8 15.8 %collective-permute-start.33 = (bf16[2,2,96,768]{3,2,1,0:T(8,128)(2,1)}, bf16[2,2,96,768]{3,2,1,0:T(8,128)(2,1)}, u32[]{:S(2)}, u32[]{:S(2)}) collective-permute-start(bf16[2,2,96,768]{3,2,1,0:T(8,128)(2,1)} %fusion.14), channel_id=1, source_target_pairs={{0,4},{4,0},{8,12},{12,8},{16,20},{20,16},{24,28},{28,24},{1,5},{5... | collective-permute-start | bytes 1769480 | tf_op jit(solution)/shard_map/ppermute | solution.py:526
  189.6 7.8 %collective-permute-start.38 = (bf16[2,2,2,2,96,384]{5,4,3,2,1,0:T(8,128)(2,1)S(1)}, bf16[2,2,2,2,96,384]{5,4,3,2,1,0:T(8,128)(2,1)S(1)}, u32[]{:S(2)}, u32[]{:S(2)}) collective-permute-start(bf16[2,2,2,2,96,384]{5,4,3,2,1,0:T(8,128)(2,1)S(1)} %bitcast.312), channel_id=1, source_target_pairs={{0,1},{1,0},{2,3},{3,2},{4,5},{5,4},{6,7},{7,6},{8,9},{9,8},{10,11... | collective-permute-start | bytes 3538952 | tf_op jit(solution)/shard_map/ppermute | solution.py:526
  191.7 25.0 %collective-permute-start.37 = (bf16[2,2,2,96,384]{4,3,2,1,0:T(8,128)(2,1)}, bf16[2,2,2,96,384]{4,3,2,1,0:T(8,128)(2,1)}, u32[]{:S(2)}, u32[]{:S(2)}) collective-permute-start(bf16[2,2,2,96,384]{4,3,2,1,0:T(8,128)(2,1)} %fusion.24), channel_id=1, source_target_pairs={{0,2},{1,3},{2,0},{3,1},{4,6},{5,7},{6,4},{7,5},{8,10},{9,11},{10,... | collective-permute-start | bytes 1769480 | tf_op jit(solution)/shard_map/ppermute | solution.py:526
  196.8 19.9 %collective-permute-start.36 = (bf16[2,192,768]{2,1,0:T(8,128)(2,1)}, bf16[2,192,768]{2,1,0:T(8,128)(2,1)}, u32[]{:S(2)}, u32[]{:S(2)}) collective-permute-start(bf16[2,192,768]{2,1,0:T(8,128)(2,1)} %pad_maximum_fusion.10), channel_id=1, source_target_pairs={{0,8},{4,12},{8,0},{12,4},{16,24},{20,28},{24,16},{28,20},{1,9},{5... | collective-permute-start | bytes 1769480 | tf_op jit(solution)/shard_map/ppermute | solution.py:526
  198.6 9.6 %copy-start.31 = (s32[768]{0:T(1024)S(1)}, s32[768]{0:T(1024)}, u32[]{:S(2)}) copy-start(s32[768]{0:T(1024)} %copy-done.30) | copy-start | bytes 9220
  198.6 9.6 %copy-start.36 = (bf16[384,768]{1,0:T(8,128)(2,1)S(1)}, bf16[384,768]{1,0:T(8,128)(2,1)}, u32[]{:S(2)}) copy-start(bf16[384,768]{1,0:T(8,128)(2,1)} %get-tuple-element.182) | copy-start | bytes 1769476
  198.6 18.1 %collective-permute-start.39 = (bf16[2,2,2,96,384]{4,3,2,1,0:T(8,128)(2,1)S(1)}, bf16[2,2,2,96,384]{4,3,2,1,0:T(8,128)(2,1)}, u32[]{:S(2)}, u32[]{:S(2)}) collective-permute-start(bf16[2,2,2,96,384]{4,3,2,1,0:T(8,128)(2,1)S(1)} %fusion.25), channel_id=1, source_target_pairs={{0,4},{4,0},{8,12},{12,8},{16,20},{20,16},{24,28},{28,24},{1,5},{5... | collective-permute-start | bytes 1769480 | tf_op jit(solution)/shard_map/ppermute | solution.py:526
  204.7 10.6 %all-to-all-start.1 = ((f32[32,1,288]{2,1,0:T(1,128)}), f32[32,1,288]{2,1,0:T(1,128)}, u32[]{:S(2)}, u32[]{:S(2)}) async-start(f32[32,1,288]{2,1,0:T(1,128)} %copy.60), calls=%async_computation.1 | async-start | bytes 98304 | tf_op jit(solution)/shard_map/all_to_all | solution.py:571
  209.8 9.4 %copy-start.8 = (bf16[2,768,384]{2,1,0:T(8,128)(2,1)S(1)}, bf16[2,768,384]{2,1,0:T(8,128)(2,1)}, u32[]{:S(2)}) copy-start(bf16[2,768,384]{2,1,0:T(8,128)(2,1)} %get-tuple-element.169) | copy-start | bytes 3538948
  218.6 6.8 %copy-start.37 = (bf16[384,768]{1,0:T(8,128)(2,1)S(1)}, bf16[384,768]{1,0:T(8,128)(2,1)}, u32[]{:S(2)}) copy-start(bf16[384,768]{1,0:T(8,128)(2,1)} %get-tuple-element.184) | copy-start | bytes 1769476
  218.6 14.1 %collective-permute-start.42 = (bf16[2,2,96,384]{3,2,1,0:T(8,128)(2,1)}, bf16[2,2,96,384]{3,2,1,0:T(8,128)(2,1)}, u32[]{:S(2)}, u32[]{:S(2)}) collective-permute-start(bf16[2,2,96,384]{3,2,1,0:T(8,128)(2,1)} %fusion.27), channel_id=1, source_target_pairs={{0,2},{1,3},{2,0},{3,1},{4,6},{5,7},{6,4},{7,5},{8,10},{9,11},{10,... | collective-permute-start | bytes 884744 | tf_op jit(solution)/shard_map/ppermute | solution.py:526
  221.1 11.6 %collective-permute-start.41 = (bf16[2,2,96,384]{3,2,1,0:T(8,128)(2,1)}, bf16[2,2,96,384]{3,2,1,0:T(8,128)(2,1)}, u32[]{:S(2)}, u32[]{:S(2)}) collective-permute-start(bf16[2,2,96,384]{3,2,1,0:T(8,128)(2,1)} %fusion.28), channel_id=1, source_target_pairs={{0,4},{4,0},{8,12},{12,8},{16,20},{20,16},{24,28},{28,24},{1,5},{5... | collective-permute-start | bytes 884744 | tf_op jit(solution)/shard_map/ppermute | solution.py:526
  223.8 16.0 %collective-permute-start.40 = (bf16[192,768]{1,0:T(8,128)(2,1)}, bf16[192,768]{1,0:T(8,128)(2,1)}, u32[]{:S(2)}, u32[]{:S(2)}) collective-permute-start(bf16[192,768]{1,0:T(8,128)(2,1)} %fusion.33), channel_id=1, source_target_pairs={{0,16},{4,20},{8,24},{12,28},{16,0},{20,4},{24,8},{28,12},{1,17},{... | collective-permute-start | bytes 884744 | tf_op jit(solution)/shard_map/ppermute | solution.py:526
  226.9 3.5 %copy-start.21 = (bf16[384,768]{1,0:T(8,128)(2,1)S(1)}, bf16[384,768]{1,0:T(8,128)(2,1)}, u32[]{:S(2)}) copy-start(bf16[384,768]{1,0:T(8,128)(2,1)} %fusion.9) | copy-start | bytes 1769476
  243.7 8.6 %collective-permute-start.43 = (bf16[96,768]{1,0:T(8,128)(2,1)S(1)}, bf16[96,768]{1,0:T(8,128)(2,1)S(1)}, u32[]{:S(2)}, u32[]{:S(2)}) collective-permute-start(bf16[96,768]{1,0:T(8,128)(2,1)S(1)} %pad_maximum_fusion.14), channel_id=1, source_target_pairs={{0,24},{4,28},{8,16},{12,20},{16,8},{20,12},{24,0},{28,4},{1,25},{... | collective-permute-start | bytes 442376 | tf_op jit(solution)/shard_map/ppermute | solution.py:526
  245.4 10.9 %collective-permute-start.44 = (bf16[96,768]{1,0:T(8,128)(2,1)S(1)}, bf16[96,768]{1,0:T(8,128)(2,1)S(1)}, u32[]{:S(2)}, u32[]{:S(2)}) collective-permute-start(bf16[96,768]{1,0:T(8,128)(2,1)S(1)} %pad_maximum_fusion.15), channel_id=1, source_target_pairs={{0,8},{4,12},{8,0},{12,4},{16,24},{20,28},{24,16},{28,20},{1,9},{5... | collective-permute-start | bytes 442376 | tf_op jit(solution)/shard_map/ppermute | solution.py:526
  245.6 11.3 %collective-permute-start.45 = (bf16[96,768]{1,0:T(8,128)(2,1)S(1)}, bf16[96,768]{1,0:T(8,128)(2,1)S(1)}, u32[]{:S(2)}, u32[]{:S(2)}) collective-permute-start(bf16[96,768]{1,0:T(8,128)(2,1)S(1)} %pad_maximum_fusion.16), channel_id=1, source_target_pairs={{0,16},{4,20},{8,24},{12,28},{16,0},{20,4},{24,8},{28,12},{1,17},{... | collective-permute-start | bytes 442376 | tf_op jit(solution)/shard_map/ppermute | solution.py:526
  (22 other events, 43.9 us)
where the time goes:
time: 260 us; the launch traced here: 259 us
  Pallas kernels  74.1 us (28%)
  waiting for transfers between devices  60.2 us (23%)
  starting transfers between devices  46.2 us (18%)
  local copies, waits for them, and re-layouts  35.9 us (14%)
  other arithmetic  31.6 us (12%)
  matrix products  9.61 us (4%)
    pallas_call x8, Pallas kernels, call(): pl.pallas_call(body, grid=grid, in_specs=in_specs, out_specs=[o[1] for o...  74.1 us
    ppermute x46, waiting for transfers between devices, flip(): piece = lax.ppermute(piece, axis, [(i, i ^ bit) for i in range(count)])  51.2 us
    ppermute x46, starting transfers between devices, flip(): piece = lax.ppermute(piece, axis, [(i, i ^ bit) for i in range(count)])  36.6 us
    unnamed x82, local copies, waits for them, and re-layouts  10.3 us
    all_to_all x2, starting transfers between devices, exchange(): return lax.all_to_all(blocks, ALL, 0, 0, tiled=True)  9.59 us
    all_to_all x2, waiting for transfers between devices, exchange(): return lax.all_to_all(blocks, ALL, 0, 0, tiled=True)  8.95 us
    convert_element_type x5, other arithmetic, shrink(): away = total(side(terms, 1, place)).astype(BF16)  7.67 us
    convert_element_type x5, other arithmetic, low_total(): return total(terms).astype(BF16)  6.82 us
  transfers between devices with their start and end apart: 48, of which 19 were waited for; matrix products, arithmetic and copies ran while one was open for 24% of the time, Pallas kernels for 29%

commit v1 on v0

--- a/solution.py
+++ b/solution.py
@@ -156,8 +156,8 @@
     cols = g_b.shape[2] // 3
     by_chunk(lambda t: g_b[t][:, :cols], per, cols)
     by_chunk(lambda t: g_b[t][:, 2 * cols :], per, cols)
-    by_chunk(lambda t: g_bu[t], out.shape[1] - (plain + 2) * per, part)
-    out[...] = jnp.concatenate(columns, axis=1)
+    by_chunk(lambda t: g_bu[t], out.shape[2] - (plain + 2) * per, part)
+    out[:, 0, :] = jnp.concatenate(columns, axis=1)
 
 
 def attention_forward(
@@ -927,8 +927,24 @@
     qk_terms = descend(qk_terms, along_y[:1], have_qk)
     vo_terms = descend(vo_terms, along_x, have_vo)
     back_z = along_z[::-1]
-    rest_terms = descend_joined(up_terms, down_terms, -2, back_z[0], have_up)
-    sums_shape = (devices, small_size)
+    pair_ud = [up_terms, down_terms]
+    for step in back_z[:-2]:
+        pair_ud = [descend(terms, [step], list(have_up)) for terms in pair_ud]
+        have_up.remove(step)
+
+    def rest_corner(i, j):
+        return jnp.concatenate(
+            [total(side(side(terms, i, 0), j, 0)) for terms in pair_ud], axis=-2
+        )
+
+    step, other = back_z[-2:]
+    rest_terms = [
+        rest_corner(0, 0),
+        flip(rest_corner(1, 1).astype(BF16), both(step, other)),
+        flip(rest_corner(1, 0).astype(BF16), step),
+        flip(rest_corner(0, 1).astype(BF16), other),
+    ]
+    sums_shape = (devices, 1, small_size)
     (sums,) = call(
         functools.partial(collect_vectors, per),
         (1,),
@@ -946,16 +962,18 @@
         turn,
     )
     layer_out = turned_back(layer_out)
-    rest_terms, qk_terms, vo_terms, swapped, (layer_out,) = lockstep(
-        rest_terms, qk_terms, vo_terms, [exchange(sums)], [layer_out]
-    )
+    qk_terms, vo_terms, swapped, (layer_out,) = lockstep(
+        qk_terms, vo_terms, [exchange(sums)], [layer_out]
+    )
+    swapped = swapped[0]
     qk_terms = descend(qk_terms, along_y[1:] + along_x, have_qk)
     vo_terms = descend(vo_terms, along_y, have_vo)
-    rest_terms = descend(rest_terms, back_z[1:], have_up)
     layer_out = unpad(layer_out)
     tokens_grad = unpad(turned_back(tokens_grad))
 
-    rest_terms, qk_terms, vo_terms = lockstep(rest_terms, qk_terms, vo_terms)
+    rest_terms[1], rest_terms[2], rest_terms[3], qk_terms[-1], vo_terms[-1] = together(
+        *rest_terms[1:], qk_terms[-1], vo_terms[-1]
+    )
     chains = [qk_terms, vo_terms]
     for step in back_z[:-2]:
         chains = [descend(terms, [step], list(have_qk)) for terms in chains]
@@ -979,7 +997,7 @@
     g_qkv = first[:, : 3 * part_cols].reshape(part_rows, 3, part_cols)
     g_out = first[:, 3 * part_cols :].reshape(n_head, -1, part_cols).transpose(1, 0, 2)
     g_out = g_out.reshape(out_weight.shape)
-    sums = jnp.sum(swapped[0], axis=0)
+    sums = jnp.sum(swapped, axis=0)[0]
 
     def part(index):
         return sums[index * per : (index + 1) * per]

time: 260 us -> 258 us (level)
  starting transfers between devices: 46.2 us -> 52.7 us
  waiting for transfers between devices: 60.2 us -> 54.6 us
  local copies, waits for them, and re-layouts: 35.9 us -> 32.1 us
    ppermute x46 -> x47, starting transfers between devices: 36.6 us -> 43.1 us  [flip(): piece = lax.ppermute(piece, axis, [(i, i ^ bit) for i in range(count)])]
    all_to_all x2, waiting for transfers between devices: 8.95 us -> 3.47 us  [exchange(): return lax.all_to_all(blocks, ALL, 0, 0, tiled=True)]
    add x2 -> x4, other arithmetic: 1.22 us -> 4.62 us  [total(): return sum((term.astype(F32) for term in terms))]
    another operation x4 -> x2, other arithmetic: 6.12 us -> 2.78 us
    unnamed x82 -> x73, local copies, waits for them, and re-layouts: 10.3 us -> 7.32 us
    convert_element_type x5 -> x4, other arithmetic: 7.67 us -> 7.21 us  [shrink(): away = total(side(terms, 1, place)).astype(BF16)]
    ppermute x46 -> x47, waiting for transfers between devices: 51.2 us -> 51.2 us  [flip(): piece = lax.ppermute(piece, axis, [(i, i ^ bit) for i in range(count)])]
  transfers between devices with their start and end apart: 48 -> 49, of which waited for: 19 -> 18; matrix products, arithmetic and copies ran while one was open for 24% -> 25% of each run, Pallas kernels for 29% -> 29%
where the time goes in v1:
time: 258 us; the launch traced here: 257 us
  Pallas kernels  74.1 us (29%)
  waiting for transfers between devices  54.6 us (21%)
  starting transfers between devices  52.7 us (20%)
  other arithmetic  33.5 us (13%)
  local copies, waits for them, and re-layouts  32.1 us (12%)
  matrix products  8.78 us (3%)
    pallas_call x8, Pallas kernels, call(): pl.pallas_call(body, grid=grid, in_specs=in_specs, out_specs=[o[1] for o...  74.1 us
    ppermute x47, waiting for transfers between devices, flip(): piece = lax.ppermute(piece, axis, [(i, i ^ bit) for i in range(count)])  51.2 us
    ppermute x47, starting transfers between devices, flip(): piece = lax.ppermute(piece, axis, [(i, i ^ bit) for i in range(count)])  43.1 us
    all_to_all x2, starting transfers between devices, exchange(): return lax.all_to_all(blocks, ALL, 0, 0, tiled=True)  9.59 us
    unnamed x73, local copies, waits for them, and re-layouts  7.32 us
    convert_element_type x4, other arithmetic, shrink(): away = total(side(terms, 1, place)).astype(BF16)  7.21 us
    convert_element_type x5, other arithmetic, low_total(): return total(terms).astype(BF16)  6.6 us
    dot_general x3, matrix products, mm(): return jnp.dot(a, b, preferred_element_type=F32)  6.55 us
  transfers between devices with their start and end apart: 49, of which 18 were waited for; matrix products, arithmetic and copies ran while one was open for 25% of the time, Pallas kernels for 29%

profile of v1, /device:TPU:0, one launch (start us, length us, event | category | flops | bytes accessed | tf_op | source)
XLA Modules:
  0.0 257.2 jit_solution(7627144573591834592)
XLA Ops:
  0.7 1.1 copy.53
  3.0 4.1 %collective-permute-start = (bf16[96,768]{1,0:T(8,128)(2,1)S(1)}, bf16[96,768]{1,0:T(8,128)(2,1)S(1)}, u32[]{:S(2)}, u32[]{:S(2)}) collective-permute-start(bf16[96,768]{1,0:T(8,128)(2,1)S(1)} %pad_maximum_fusion.14), channel_id=1, source_target_pairs={{0,16},{4,20},{8,24},{12,28},{16,0},{20,4},{24,8},{28,12},{1,17},{... | collective-permute-start | bytes 442376 | tf_op jit(solution)/shard_map/ppermute | solution.py:526
  7.1 1.6 collective-permute-start.1
  12.3 6.1 %all-to-all-start = ((bf16[32,2,144]{2,1,0:T(2,128)(2,1)}), bf16[32,2,144]{2,1,0:T(2,128)(2,1)S(1)}, u32[]{:S(2)}, u32[]{:S(2)}) async-start(bf16[32,2,144]{2,1,0:T(2,128)(2,1)} %reshape.809), calls=%async_computation | async-start | bytes 65536 | tf_op jit(solution)/shard_map/all_to_all | solution.py:571
  18.9 1.6 fusion.7.x
  20.5 1.6 fusion.8.top
  22.1 3.5 %all-to-all-done = bf16[32,2,144]{2,1,0:T(2,128)(2,1)S(1)} async-done(((bf16[32,2,144]{2,1,0:T(2,128)(2,1)}), bf16[32,2,144]{2,1,0:T(2,128)(2,1)S(1)}, u32[]{:S(2)}, u32[]{:S(2)}) %all-to-all-start) | async-done | bytes 18464 | tf_op jit(solution)/shard_map/all_to_all | solution.py:571
  27.8 1.4 fusion.3.turn
  30.8 2.5 shard_map.254
  33.3 2.4 collective-permute-done.4
  36.0 8.9 %collective-permute-done.5 = bf16[192,768]{1,0:T(8,128)(2,1)S(1)} collective-permute-done((bf16[192,768]{1,0:T(8,128)(2,1)S(1)}, bf16[192,768]{1,0:T(8,128)(2,1)S(1)}, u32[]{:S(2)}, u32[]{:S(2)}) %collective-permute-start.5) | collective-permute-done | bytes 294944 | tf_op jit(solution)/shard_map/ppermute | solution.py:526
  44.9 1.5 collective-permute-start.7
  47.5 12.7 %collective-permute-done.7 = bf16[2,2,2,96,384]{4,3,2,1,0:T(8,128)(2,1)S(1)} collective-permute-done((bf16[2,2,2,96,384]{4,3,2,1,0:T(8,128)(2,1)S(1)}, bf16[2,2,2,96,384]{4,3,2,1,0:T(8,128)(2,1)S(1)}, u32[]{:S(2)}, u32[]{:S(2)}) %collective-permute-start.7) | collective-permute-done | bytes 589856 | tf_op jit(solution)/shard_map/ppermute | solution.py:526
  61.4 1.2 pad_maximum_fusion.5
  64.6 1.4 collective-permute-start.12
  66.7 1.3 collective-permute-start.9
  68.0 1.2 dynamic_slice.3.lengths
  70.2 1.9 copy.68
  72.1 3.1 %reshape.693 = bf16[32,24,768]{2,1,0:T(8,128)(2,1)S(1)} reshape(bf16[32,24,4,192]{3,2,1,0:T(4,128)(2,1)} %bitcast.325) | data formatting | bytes 2359296 | tf_op jit(solution)/shard_map/reshape | solution.py:709
  75.3 1.6 gather_fusion
  76.9 3.4 %fusion.6.w_out.rest_12_ = bf16[768,768]{1,0:T(8,128)(2,1)} fusion(bf16[768,768]{1,0:T(8,128)(2,1)} %bitcast.344, s32[768]{0:T(1024)S(1)} %fusion.45), kind=kOutput, calls=%fused_computation.12 | convolution fusion | flops 907149312 | bytes 2362368 | tf_op jit(solution)/shard_map/dot_general | solution.py:20
  80.4 10.3 %shard_map.255 = (bf16[4,384,192]{2,1,0:T(8,128)(2,1)}, bf16[4,384,192]{2,1,0:T(8,128)(2,1)}, bf16[4,384,192]{2,1,0:T(8,128)(2,1)}, f32[4,6,192,192]{3,2,1,0:T(8,128)}, bf16[4,384,192]{2,1,0:T(8,128)(2,1)}) custom-call(s32[2]{0:T(128)} %dynamic_slice.3.lengths, s32[4]{0:T(128)} %get-tuple-element.294.order.rest_9_, bf16[384,768]{1,0:T(8,128)(2,1)} %fusion.7.x, ...), custom_call_target="tpu_custom_call" | custom-call | flops 226492416 | bytes 884736 | tf_op jit(solution)/shard_map/pallas_call | solution.py:477
  90.7 5.1 %shard_map.256 = (f32[384,768]{1,0:T(8,128)}, bf16[384,768]{1,0:T(8,128)(2,1)}, bf16[768,384]{1,0:T(8,128)(2,1)}, bf16[768,384]{1,0:T(8,128)(2,1)}) custom-call(s32[4]{0:T(128)} %get-tuple-element.294.order.rest_9_, bf16[384,768]{1,0:T(8,128)(2,1)} %fusion.7.x, bf16[4,384,192]{2,1,0:T(8,128)(2,1)} %get-tuple-element.120.ctx, ...), custom_call_target="tpu_custom_call" | custom-call | flops 56623104 | bytes 589824 | tf_op jit(solution)/shard_map/pallas_call | solution.py:477
  98.0 1.1 collective-permute-start.24
  102.3 12.0 %shard_map.257 = (bf16[768,768]{1,0:T(8,128)(2,1)}, bf16[768,768]{1,0:T(8,128)(2,1)}, bf16[768,768]{1,0:T(8,128)(2,1)}, bf16[768,768]{1,0:T(8,128)(2,1)}, f32[2,...) custom-call(bf16[384,768]{1,0:T(8,128)(2,1)} %get-tuple-element.123.hidden, ...), custom_call_target="tpu_custom_call" | custom-call | flops 679477248 | bytes 737280 | tf_op jit(solution)/shard_map/pallas_call | solution.py:477
  115.3 1.7 collective-permute-done.26
  118.7 14.4 %shard_map.258 = (bf16[768,768]{1,0:T(8,128)(2,1)}, bf16[768,768]{1,0:T(8,128)(2,1)}, bf16[768,768]{1,0:T(8,128)(2,1)}, bf16[768,768]{1,0:T(8,128)(2,1)}, f32[2,...) custom-call(bf16[384,768]{1,0:T(8,128)(2,1)} %get-tuple-element.123., ...), custom_call_target="tpu_custom_call" | custom-call | flops 679477248 | bytes 737280 | tf_op jit(solution)/shard_map/pallas_call | solution.py:477
  135.0 1.2 copy-done.8
  139.5 1.1 fusion.13
  140.7 1.1 collective-permute-start.29
  142.9 1.1 slice.643
  144.0 21.0 %shard_map.259 = (bf16[384,768]{1,0:T(8,128)(2,1)}, bf16[2,768,384]{2,1,0:T(8,128)(2,1)}, bf16[2,768,384]{2,1,0:T(8,128)(2,1)}, bf16[2,768,192]{2,1,0:T(8,128)(2...) custom-call(bf16[384,768]{1,0:T(8,128)(2,1)} %fusion.7.x, ...), custom_call_target="tpu_custom_call" | custom-call | flops 452984832 | bytes 884736 | tf_op jit(solution)/shard_map/pallas_call | solution.py:477
  165.0 3.7 %collective-permute-done.32 = bf16[2,2,96,768]{3,2,1,0:T(8,128)(2,1)} collective-permute-done((bf16[2,2,96,768]{3,2,1,0:T(8,128)(2,1)S(1)}, bf16[2,2,96,768]{3,2,1,0:T(8,128)(2,1)}, u32[]{:S(2)}, u32[]{:S(2)}) %collective-permute-start.32) | collective-permute-done | bytes 589856 | tf_op jit(solution)/shard_map/ppermute | solution.py:526
  168.7 2.1 fusion.12
  170.8 1.1 collective-permute-start.34
  171.9 2.3 fusion.18
  175.1 5.8 %shard_map.260 = bf16[768,768]{1,0:T(8,128)(2,1)} custom-call(s32[4]{0:T(128)} %get-tuple-element.294.order.rest_9_, bf16[4,384,192]{2,1,0:T(8,128)(2,1)} %get-tuple-element.120.ctx, bf16[384,768]{1,0:T(8,128)(2,1)} %get-tuple-element.167.grad_attn, bf16[768,768]{1,0:T(8,128)(2,1)} %fusion.3.turn), custom_call_target="tpu_custom_call" | custom-call | tf_op jit(solution)/shard_map/pallas_call | solution.py:477
  181.0 1.9 gather_fusion.1
  182.9 1.4 reshape.717
  185.7 1.5 pad_maximum_fusion.4
  187.7 2.2 collective-permute-done.33
  190.6 1.5 fusion.9
  192.2 3.0 %shard_map.261 = f32[32,1,288]{2,1,0:T(1,128)} custom-call(s32[4]{0:T(128)} %get-tuple-element.294.order.rest_9_, f32[2,768]{1,0:T(2,128)} %get-tuple-element.174.sums_one, f32[4,768]{1,0:T(4,128)} %get-tuple-element.175.sums_two, f32[4,1,576]{2,1,0:T(1,128)} %get-tuple-element.176.g_b, f32[4,1,768]{2,1,0:T(1,128)} %reshape.722.g_bu, ...), custom_call_target="tpu_custom_call" | custom-call | bytes 294912 | tf_op jit(solution)/shard_map/pallas_call | solution.py:477
  195.2 3.5 %all-to-all-start.1 = ((f32[32,1,288]{2,1,0:T(1,128)}), f32[32,1,288]{2,1,0:T(1,128)}, u32[]{:S(2)}, u32[]{:S(2)}) async-start(f32[32,1,288]{2,1,0:T(1,128)} %shard_map.261), calls=%async_computation.1 | async-start | bytes 98304 | tf_op jit(solution)/shard_map/all_to_all | solution.py:571
  200.4 1.3 fusion.24
  201.7 1.4 collective-permute-start.36
  203.1 1.9 convert_add_fusion.11
  205.0 2.2 fusion.25
  207.2 1.5 collective-permute-start.38
  208.7 1.4 convert_add_fusion.8
  210.8 2.5 collective-permute-start.41
  214.0 1.5 collective-permute-start.40
  217.4 5.1 %collective-permute-done.38 = bf16[2,2,2,96,384]{4,3,2,1,0:T(8,128)(2,1)} collective-permute-done((bf16[2,2,2,96,384]{4,3,2,1,0:T(8,128)(2,1)}, bf16[2,2,2,96,384]{4,3,2,1,0:T(8,128)(2,1)}, u32[]{:S(2)}, u32[]{:S(2)}) %collective-permute-start.38) | collective-permute-done | bytes 589856 | tf_op jit(solution)/shard_map/ppermute | solution.py:526
  222.6 1.9 fusion.29
  225.3 1.9 fusion.30
  227.1 1.2 collective-permute-start.42
  232.0 2.2 collective-permute-done.39
  235.2 1.4 fusion.44
  236.6 1.4 fusion.43
  238.0 3.1 %collective-permute-start.44 = (bf16[96,768]{1,0:T(8,128)(2,1)S(1)}, bf16[96,768]{1,0:T(8,128)(2,1)S(1)}, u32[]{:S(2)}, u32[]{:S(2)}) collective-permute-start(bf16[96,768]{1,0:T(8,128)(2,1)S(1)} %pad_maximum_fusion.15), channel_id=1, source_target_pairs={{0,24},{4,28},{8,16},{12,20},{16,8},{20,12},{24,0},{28,4},{1,25},{... | collective-permute-start | bytes 442376 | tf_op jit(solution)/shard_map/ppermute | solution.py:526
  241.1 4.4 %collective-permute-start.45 = (bf16[96,768]{1,0:T(8,128)(2,1)S(1)}, bf16[96,768]{1,0:T(8,128)(2,1)S(1)}, u32[]{:S(2)}, u32[]{:S(2)}) collective-permute-start(bf16[96,768]{1,0:T(8,128)(2,1)S(1)} %pad_maximum_fusion.16), channel_id=1, source_target_pairs={{0,8},{4,12},{8,0},{12,4},{16,24},{20,28},{24,16},{28,20},{1,9},{5... | collective-permute-start | bytes 442376 | tf_op jit(solution)/shard_map/ppermute | solution.py:526
  245.6 1.3 fusion.28
  247.7 2.2 collective-permute-done.45
  249.9 5.3 %collective-permute-done.46 = bf16[96,768]{1,0:T(8,128)(2,1)S(1)} collective-permute-done((bf16[96,768]{1,0:T(8,128)(2,1)S(1)}, bf16[96,768]{1,0:T(8,128)(2,1)S(1)}, u32[]{:S(2)}, u32[]{:S(2)}) %collective-permute-start.46) | collective-permute-done | bytes 147488 | tf_op jit(solution)/shard_map/ppermute | solution.py:526
  (216 shorter events, 46.5 us)
Async XLA Ops:
  0.6 17.9 %copy-start.24 = (bf16[370,768]{1,0:T(8,128)(2,1)S(1)}, bf16[370,768]{1,0:T(8,128)(2,1)}, u32[]{:S(2)}) copy-start(bf16[370,768]{1,0:T(8,128)(2,1)} %param.15) | copy-start | bytes 1704964
  1.8 16.9 %copy-start.25 = (bf16[370,768]{1,0:T(8,128)(2,1)S(1)}, bf16[370,768]{1,0:T(8,128)(2,1)}, u32[]{:S(2)}) copy-start(bf16[370,768]{1,0:T(8,128)(2,1)} %param.29) | copy-start | bytes 1704964
  3.0 23.4 %collective-permute-start = (bf16[96,768]{1,0:T(8,128)(2,1)S(1)}, bf16[96,768]{1,0:T(8,128)(2,1)S(1)}, u32[]{:S(2)}, u32[]{:S(2)}) collective-permute-start(bf16[96,768]{1,0:T(8,128)(2,1)S(1)} %pad_maximum_fusion.14), channel_id=1, source_target_pairs={{0,16},{4,20},{8,24},{12,28},{16,0},{20,4},{24,8},{28,12},{1,17},{... | collective-permute-start | bytes 442376 | tf_op jit(solution)/shard_map/ppermute | solution.py:526
  7.1 19.2 %collective-permute-start.1 = (bf16[96,768]{1,0:T(8,128)(2,1)S(1)}, bf16[96,768]{1,0:T(8,128)(2,1)S(1)}, u32[]{:S(2)}, u32[]{:S(2)}) collective-permute-start(bf16[96,768]{1,0:T(8,128)(2,1)S(1)} %pad_maximum_fusion.14), channel_id=1, source_target_pairs={{0,8},{4,12},{8,0},{12,4},{16,24},{20,28},{24,16},{28,20},{1,9},{5... | collective-permute-start | bytes 442376 | tf_op jit(solution)/shard_map/ppermute | solution.py:526
  8.7 17.7 %collective-permute-start.2 = (bf16[96,768]{1,0:T(8,128)(2,1)S(1)}, bf16[96,768]{1,0:T(8,128)(2,1)S(1)}, u32[]{:S(2)}, u32[]{:S(2)}) collective-permute-start(bf16[96,768]{1,0:T(8,128)(2,1)S(1)} %pad_maximum_fusion.14), channel_id=1, source_target_pairs={{0,24},{4,28},{8,16},{12,20},{16,8},{20,12},{24,0},{28,4},{1,25},{... | collective-permute-start | bytes 442376 | tf_op jit(solution)/shard_map/ppermute | solution.py:526
  12.3 13.3 %all-to-all-start = ((bf16[32,2,144]{2,1,0:T(2,128)(2,1)}), bf16[32,2,144]{2,1,0:T(2,128)(2,1)S(1)}, u32[]{:S(2)}, u32[]{:S(2)}) async-start(bf16[32,2,144]{2,1,0:T(2,128)(2,1)} %reshape.809), calls=%async_computation | async-start | bytes 65536 | tf_op jit(solution)/shard_map/all_to_all | solution.py:571
  26.6 9.1 %collective-permute-start.4 = (bf16[2,2,96,384]{3,2,1,0:T(8,128)(2,1)S(1)}, bf16[2,2,96,384]{3,2,1,0:T(8,128)(2,1)S(1)}, u32[]{:S(2)}, u32[]{:S(2)}) collective-permute-start(bf16[2,2,96,384]{3,2,1,0:T(8,128)(2,1)S(1)} %get-tuple-element.280), channel_id=1, source_target_pairs={{0,2},{1,3},{2,0},{3,1},{4,6},{5,7},{6,4},{7,5},{8,10},{9,11},{10,... | collective-permute-start | bytes 884744 | tf_op jit(solution)/shard_map/ppermute | solution.py:526
  27.1 8.7 %collective-permute-start.3 = (bf16[2,2,96,384]{3,2,1,0:T(8,128)(2,1)S(1)}, bf16[2,2,96,384]{3,2,1,0:T(8,128)(2,1)S(1)}, u32[]{:S(2)}, u32[]{:S(2)}) collective-permute-start(bf16[2,2,96,384]{3,2,1,0:T(8,128)(2,1)S(1)} %get-tuple-element.281), channel_id=1, source_target_pairs={{0,4},{4,0},{8,12},{12,8},{16,20},{20,16},{24,28},{28,24},{1,5},{5... | collective-permute-start | bytes 884744 | tf_op jit(solution)/shard_map/ppermute | solution.py:526
  29.3 15.6 %collective-permute-start.5 = (bf16[192,768]{1,0:T(8,128)(2,1)S(1)}, bf16[192,768]{1,0:T(8,128)(2,1)S(1)}, u32[]{:S(2)}, u32[]{:S(2)}) collective-permute-start(bf16[192,768]{1,0:T(8,128)(2,1)S(1)} %pad_maximum_fusion.10), channel_id=1, source_target_pairs={{0,16},{4,20},{8,24},{12,28},{16,0},{20,4},{24,8},{28,12},{1,17},{... | collective-permute-start | bytes 884744 | tf_op jit(solution)/shard_map/ppermute | solution.py:526
  44.9 15.3 %collective-permute-start.7 = (bf16[2,2,2,96,384]{4,3,2,1,0:T(8,128)(2,1)S(1)}, bf16[2,2,2,96,384]{4,3,2,1,0:T(8,128)(2,1)S(1)}, u32[]{:S(2)}, u32[]{:S(2)}) collective-permute-start(bf16[2,2,2,96,384]{4,3,2,1,0:T(8,128)(2,1)S(1)} %pad_maximum_fusion.8), channel_id=1, source_target_pairs={{0,4},{4,0},{8,12},{12,8},{16,20},{20,16},{24,28},{28,24},{1,5},{5... | collective-permute-start | bytes 1769480 | tf_op jit(solution)/shard_map/ppermute | solution.py:526
  46.4 14.9 %collective-permute-start.8 = (bf16[2,192,768]{2,1,0:T(8,128)(2,1)S(1)}, bf16[2,192,768]{2,1,0:T(8,128)(2,1)S(1)}, u32[]{:S(2)}, u32[]{:S(2)}) collective-permute-start(bf16[2,192,768]{2,1,0:T(8,128)(2,1)S(1)} %pad_maximum_fusion.9), channel_id=1, source_target_pairs={{0,8},{4,12},{8,0},{12,4},{16,24},{20,28},{24,16},{28,20},{1,9},{5... | collective-permute-start | bytes 1769480 | tf_op jit(solution)/shard_map/ppermute | solution.py:526
  46.4 16.1 %collective-permute-start.6 = (bf16[2,2,2,96,384]{4,3,2,1,0:T(8,128)(2,1)S(1)}, bf16[2,2,2,96,384]{4,3,2,1,0:T(8,128)(2,1)S(1)}, u32[]{:S(2)}, u32[]{:S(2)}) collective-permute-start(bf16[2,2,2,96,384]{4,3,2,1,0:T(8,128)(2,1)S(1)} %pad_maximum_fusion.7), channel_id=1, source_target_pairs={{0,2},{1,3},{2,0},{3,1},{4,6},{5,7},{6,4},{7,5},{8,10},{9,11},{10,... | collective-permute-start | bytes 1769480 | tf_op jit(solution)/shard_map/ppermute | solution.py:526
  60.5 8.7 %copy-start = (bf16[2,2,2,2,96,384]{5,4,3,2,1,0:T(8,128)(2,1)}, bf16[2,2,2,2,96,384]{5,4,3,2,1,0:T(8,128)(2,1)S(1)}, u32[]{:S(2)}) copy-start(bf16[2,2,2,2,96,384]{5,4,3,2,1,0:T(8,128)(2,1)S(1)} %copy.56) | copy-start | bytes 3538948
  62.7 7.2 %copy-start.1 = (bf16[2,768,384]{2,1,0:T(8,128)(2,1)}, bf16[2,768,384]{2,1,0:T(8,128)(2,1)S(1)}, u32[]{:S(2)}) copy-start(bf16[2,768,384]{2,1,0:T(8,128)(2,1)S(1)} %pad_maximum_fusion.1.qk_near) | copy-start | bytes 3538948
  62.7 4.0 %collective-permute-start.14 = (bf16[2,768,384]{2,1,0:T(8,128)(2,1)S(1)}, bf16[2,768,384]{2,1,0:T(8,128)(2,1)S(1)}, u32[]{:S(2)}, u32[]{:S(2)}) collective-permute-start(bf16[2,768,384]{2,1,0:T(8,128)(2,1)S(1)} %bitcast.319), channel_id=1, source_target_pairs={{0,1},{1,0},{2,3},{3,2},{4,5},{5,4},{6,7},{7,6},{8,9},{9,8},{10,11... | collective-permute-start | bytes 3538952 | tf_op jit(solution)/shard_map/ppermute | solution.py:526
  62.7 14.2 %collective-permute-start.13 = (bf16[2,768,384]{2,1,0:T(8,128)(2,1)S(1)}, bf16[2,768,384]{2,1,0:T(8,128)(2,1)}, u32[]{:S(2)}, u32[]{:S(2)}) collective-permute-start(bf16[2,768,384]{2,1,0:T(8,128)(2,1)S(1)} %pad_maximum_fusion.1.qk_near), channel_id=1, source_target_pairs={{0,1},{1,0},{2,3},{3,2},{4,5},{5,4},{6,7},{7,6},{8,9},{9,8},{10,11... | collective-permute-start | bytes 3538952 | tf_op jit(solution)/shard_map/ppermute | solution.py:526
  63.9 31.9 %collective-permute-start.10 = (bf16[2,2,96,768]{3,2,1,0:T(8,128)(2,1)}, bf16[2,2,96,768]{3,2,1,0:T(8,128)(2,1)}, u32[]{:S(2)}, u32[]{:S(2)}) collective-permute-start(bf16[2,2,96,768]{3,2,1,0:T(8,128)(2,1)} %get-tuple-element.114), channel_id=1, source_target_pairs={{0,4},{4,0},{8,12},{12,8},{16,20},{20,16},{24,28},{28,24},{1,5},{5... | collective-permute-start | bytes 1769480 | tf_op jit(solution)/shard_map/ppermute | solution.py:526
  64.6 31.8 %collective-permute-start.12 = (bf16[2,2,96,768]{3,2,1,0:T(8,128)(2,1)}, bf16[2,2,96,768]{3,2,1,0:T(8,128)(2,1)}, u32[]{:S(2)}, u32[]{:S(2)}) collective-permute-start(bf16[2,2,96,768]{3,2,1,0:T(8,128)(2,1)} %get-tuple-element.114), channel_id=1, source_target_pairs={{0,2},{1,3},{2,0},{3,1},{4,6},{5,7},{6,4},{7,5},{8,10},{9,11},{10,... | collective-permute-start | bytes 1769480 | tf_op jit(solution)/shard_map/ppermute | solution.py:526
  66.0 30.4 %collective-permute-start.11 = (bf16[2,2,96,768]{3,2,1,0:T(8,128)(2,1)}, bf16[2,2,96,768]{3,2,1,0:T(8,128)(2,1)}, u32[]{:S(2)}, u32[]{:S(2)}) collective-permute-start(bf16[2,2,96,768]{3,2,1,0:T(8,128)(2,1)} %get-tuple-element.113), channel_id=1, source_target_pairs={{0,2},{1,3},{2,0},{3,1},{4,6},{5,7},{6,4},{7,5},{8,10},{9,11},{10,... | collective-permute-start | bytes 1769480 | tf_op jit(solution)/shard_map/ppermute | solution.py:526
  66.7 29.8 %collective-permute-start.9 = (bf16[2,2,96,768]{3,2,1,0:T(8,128)(2,1)}, bf16[2,2,96,768]{3,2,1,0:T(8,128)(2,1)}, u32[]{:S(2)}, u32[]{:S(2)}) collective-permute-start(bf16[2,2,96,768]{3,2,1,0:T(8,128)(2,1)} %get-tuple-element.113), channel_id=1, source_target_pairs={{0,4},{4,0},{8,12},{12,8},{16,20},{20,16},{24,28},{28,24},{1,5},{5... | collective-permute-start | bytes 1769480 | tf_op jit(solution)/shard_map/ppermute | solution.py:526
  76.9 20.1 %collective-permute-start.15 = (bf16[2,2,96,768]{3,2,1,0:T(8,128)(2,1)S(1)}, bf16[2,2,96,768]{3,2,1,0:T(8,128)(2,1)S(1)}, u32[]{:S(2)}, u32[]{:S(2)}) collective-permute-start(bf16[2,2,96,768]{3,2,1,0:T(8,128)(2,1)S(1)} %copy-done.4), channel_id=1, source_target_pairs={{0,1},{1,0},{2,3},{3,2},{4,5},{5,4},{6,7},{7,6},{8,9},{9,8},{10,11... | collective-permute-start | bytes 1769480 | tf_op jit(solution)/shard_map/ppermute | solution.py:526
  90.7 5.2 %copy-start.3 = (bf16[2,2,96,768]{3,2,1,0:T(8,128)(2,1)S(1)}, bf16[2,2,96,768]{3,2,1,0:T(8,128)(2,1)}, u32[]{:S(2)}) copy-start(bf16[2,2,96,768]{3,2,1,0:T(8,128)(2,1)} %get-tuple-element.114) | copy-start | bytes 1769476
  95.8 2.2 collective-permute-start.17
  96.4 2.7 %collective-permute-start.16 = (bf16[2,2,96,768]{3,2,1,0:T(8,128)(2,1)}, bf16[2,2,96,768]{3,2,1,0:T(8,128)(2,1)S(1)}, u32[]{:S(2)}, u32[]{:S(2)}) collective-permute-start(bf16[2,2,96,768]{3,2,1,0:T(8,128)(2,1)} %collective-permute-done.9), channel_id=1, source_target_pairs={{0,1},{1,0},{2,3},{3,2},{4,5},{5,4},{6,7},{7,6},{8,9},{9,8},{10,11... | collective-permute-start | bytes 1769480 | tf_op jit(solution)/shard_map/ppermute | solution.py:526
  96.5 5.0 %collective-permute-start.18 = (bf16[2,2,96,768]{3,2,1,0:T(8,128)(2,1)}, bf16[2,2,96,768]{3,2,1,0:T(8,128)(2,1)S(1)}, u32[]{:S(2)}, u32[]{:S(2)}) collective-permute-start(bf16[2,2,96,768]{3,2,1,0:T(8,128)(2,1)} %collective-permute-done.10), channel_id=1, source_target_pairs={{0,1},{1,0},{2,3},{3,2},{4,5},{5,4},{6,7},{7,6},{8,9},{9,8},{10,11... | collective-permute-start | bytes 1769480 | tf_op jit(solution)/shard_map/ppermute | solution.py:526
  97.0 4.5 %collective-permute-start.19 = (bf16[2,2,96,768]{3,2,1,0:T(8,128)(2,1)}, bf16[2,2,96,768]{3,2,1,0:T(8,128)(2,1)}, u32[]{:S(2)}, u32[]{:S(2)}) collective-permute-start(bf16[2,2,96,768]{3,2,1,0:T(8,128)(2,1)} %collective-permute-done.11), channel_id=1, source_target_pairs={{0,1},{1,0},{2,3},{3,2},{4,5},{5,4},{6,7},{7,6},{8,9},{9,8},{10,11... | collective-permute-start | bytes 1769480 | tf_op jit(solution)/shard_map/ppermute | solution.py:526
  97.1 4.4 %copy-start.14 = (bf16[2,2,96,768]{3,2,1,0:T(8,128)(2,1)}, bf16[2,2,96,768]{3,2,1,0:T(8,128)(2,1)S(1)}, u32[]{:S(2)}) copy-start(bf16[2,2,96,768]{3,2,1,0:T(8,128)(2,1)S(1)} %collective-permute-done.15) | copy-start | bytes 1769476
  97.1 4.4 %collective-permute-start.20 = (bf16[2,2,96,768]{3,2,1,0:T(8,128)(2,1)}, bf16[2,2,96,768]{3,2,1,0:T(8,128)(2,1)S(1)}, u32[]{:S(2)}, u32[]{:S(2)}) collective-permute-start(bf16[2,2,96,768]{3,2,1,0:T(8,128)(2,1)} %collective-permute-done.12), channel_id=1, source_target_pairs={{0,1},{1,0},{2,3},{3,2},{4,5},{5,4},{6,7},{7,6},{8,9},{9,8},{10,11... | collective-permute-start | bytes 1769480 | tf_op jit(solution)/shard_map/ppermute | solution.py:526
  98.0 3.5 %copy-start.15 = (bf16[2,2,96,768]{3,2,1,0:T(8,128)(2,1)}, bf16[2,2,96,768]{3,2,1,0:T(8,128)(2,1)S(1)}, u32[]{:S(2)}) copy-start(bf16[2,2,96,768]{3,2,1,0:T(8,128)(2,1)S(1)} %collective-permute-done.17) | copy-start | bytes 1769476
  98.0 16.2 %collective-permute-start.24 = (bf16[2,2,96,768]{3,2,1,0:T(8,128)(2,1)}, bf16[2,2,96,768]{3,2,1,0:T(8,128)(2,1)}, u32[]{:S(2)}, u32[]{:S(2)}) collective-permute-start(bf16[2,2,96,768]{3,2,1,0:T(8,128)(2,1)} %collective-permute-done.9), channel_id=1, source_target_pairs={{0,2},{1,3},{2,0},{3,1},{4,6},{5,7},{6,4},{7,5},{8,10},{9,11},{10,... | collective-permute-start | bytes 1769480 | tf_op jit(solution)/shard_map/ppermute | solution.py:526
  99.2 15.6 %collective-permute-start.25 = (bf16[2,2,96,768]{3,2,1,0:T(8,128)(2,1)}, bf16[2,2,96,768]{3,2,1,0:T(8,128)(2,1)}, u32[]{:S(2)}, u32[]{:S(2)}) collective-permute-start(bf16[2,2,96,768]{3,2,1,0:T(8,128)(2,1)} %collective-permute-done.12), channel_id=1, source_target_pairs={{0,4},{4,0},{8,12},{12,8},{16,20},{20,16},{24,28},{28,24},{1,5},{5... | collective-permute-start | bytes 1769480 | tf_op jit(solution)/shard_map/ppermute | solution.py:526
  101.5 12.8 %copy-start.21 = (bf16[2,2,96,768]{3,2,1,0:T(8,128)(2,1)}, bf16[2,2,96,768]{3,2,1,0:T(8,128)(2,1)S(1)}, u32[]{:S(2)}) copy-start(bf16[2,2,96,768]{3,2,1,0:T(8,128)(2,1)S(1)} %collective-permute-done.20) | copy-start | bytes 1769476
  114.8 2.2 collective-permute-start.26
  114.8 3.1 %collective-permute-start.27 = (bf16[2,2,96,768]{3,2,1,0:T(8,128)(2,1)}, bf16[2,2,96,768]{3,2,1,0:T(8,128)(2,1)S(1)}, u32[]{:S(2)}, u32[]{:S(2)}) collective-permute-start(bf16[2,2,96,768]{3,2,1,0:T(8,128)(2,1)} %collective-permute-done.25), channel_id=1, source_target_pairs={{0,1},{1,0},{2,3},{3,2},{4,5},{5,4},{6,7},{7,6},{8,9},{9,8},{10,11... | collective-permute-start | bytes 1769480 | tf_op jit(solution)/shard_map/ppermute | solution.py:526
  115.3 21.0 %collective-permute-start.22 = (bf16[2,2,2,96,768]{4,3,2,1,0:T(8,128)(2,1)}, bf16[2,2,2,96,768]{4,3,2,1,0:T(8,128)(2,1)S(1)}, u32[]{:S(2)}, u32[]{:S(2)}) collective-permute-start(bf16[2,2,2,96,768]{4,3,2,1,0:T(8,128)(2,1)} %bitcast.379), channel_id=1, source_target_pairs={{0,1},{1,0},{2,3},{3,2},{4,5},{5,4},{6,7},{7,6},{8,9},{9,8},{10,11... | collective-permute-start | bytes 3538952 | tf_op jit(solution)/shard_map/ppermute | solution.py:526
  133.1 4.4 %collective-permute-start.30 = (bf16[2,2,2,96,768]{4,3,2,1,0:T(8,128)(2,1)}, bf16[2,2,2,96,768]{4,3,2,1,0:T(8,128)(2,1)S(1)}, u32[]{:S(2)}, u32[]{:S(2)}) collective-permute-start(bf16[2,2,2,96,768]{4,3,2,1,0:T(8,128)(2,1)} %bitcast.382), channel_id=1, source_target_pairs={{0,1},{1,0},{2,3},{3,2},{4,5},{5,4},{6,7},{7,6},{8,9},{9,8},{10,11... | collective-permute-start | bytes 3538952 | tf_op jit(solution)/shard_map/ppermute | solution.py:526
  133.3 6.3 %collective-permute-start.28 = (bf16[2,2,2,96,768]{4,3,2,1,0:T(8,128)(2,1)}, bf16[2,2,2,96,768]{4,3,2,1,0:T(8,128)(2,1)S(1)}, u32[]{:S(2)}, u32[]{:S(2)}) collective-permute-start(bf16[2,2,2,96,768]{4,3,2,1,0:T(8,128)(2,1)} %bitcast.381), channel_id=1, source_target_pairs={{0,1},{1,0},{2,3},{3,2},{4,5},{5,4},{6,7},{7,6},{8,9},{9,8},{10,11... | collective-permute-start | bytes 3538952 | tf_op jit(solution)/shard_map/ppermute | solution.py:526
  134.8 37.1 %collective-permute-start.21 = (bf16[2,2,2,96,768]{4,3,2,1,0:T(8,128)(2,1)}, bf16[2,2,2,96,768]{4,3,2,1,0:T(8,128)(2,1)}, u32[]{:S(2)}, u32[]{:S(2)}) collective-permute-start(bf16[2,2,2,96,768]{4,3,2,1,0:T(8,128)(2,1)} %bitcast.378), channel_id=1, source_target_pairs={{0,1},{1,0},{2,3},{3,2},{4,5},{5,4},{6,7},{7,6},{8,9},{9,8},{10,11... | collective-permute-start | bytes 3538952 | tf_op jit(solution)/shard_map/ppermute | solution.py:526
  136.5 28.4 %collective-permute-start.23 = (bf16[2,2,96,768]{3,2,1,0:T(8,128)(2,1)S(1)}, bf16[2,2,96,768]{3,2,1,0:T(8,128)(2,1)}, u32[]{:S(2)}, u32[]{:S(2)}) collective-permute-start(bf16[2,2,96,768]{3,2,1,0:T(8,128)(2,1)S(1)} %fusion.16), channel_id=1, source_target_pairs={{0,4},{4,0},{8,12},{12,8},{16,20},{20,16},{24,28},{28,24},{1,5},{5... | collective-permute-start | bytes 1769480 | tf_op jit(solution)/shard_map/ppermute | solution.py:526
  138.4 26.5 %collective-permute-start.31 = (bf16[2,2,96,768]{3,2,1,0:T(8,128)(2,1)}, bf16[2,2,96,768]{3,2,1,0:T(8,128)(2,1)}, u32[]{:S(2)}, u32[]{:S(2)}) collective-permute-start(bf16[2,2,96,768]{3,2,1,0:T(8,128)(2,1)} %fusion.14), channel_id=1, source_target_pairs={{0,4},{4,0},{8,12},{12,8},{16,20},{20,16},{24,28},{28,24},{1,5},{5... | collective-permute-start | bytes 1769480 | tf_op jit(solution)/shard_map/ppermute | solution.py:526
  140.7 24.3 %collective-permute-start.29 = (bf16[2,2,96,768]{3,2,1,0:T(8,128)(2,1)}, bf16[2,2,96,768]{3,2,1,0:T(8,128)(2,1)}, u32[]{:S(2)}, u32[]{:S(2)}) collective-permute-start(bf16[2,2,96,768]{3,2,1,0:T(8,128)(2,1)} %get-tuple-element.271), channel_id=1, source_target_pairs={{0,2},{1,3},{2,0},{3,1},{4,6},{5,7},{6,4},{7,5},{8,10},{9,11},{10,... | collective-permute-start | bytes 1769480 | tf_op jit(solution)/shard_map/ppermute | solution.py:526
  141.8 26.9 %collective-permute-start.32 = (bf16[2,2,96,768]{3,2,1,0:T(8,128)(2,1)S(1)}, bf16[2,2,96,768]{3,2,1,0:T(8,128)(2,1)}, u32[]{:S(2)}, u32[]{:S(2)}) collective-permute-start(bf16[2,2,96,768]{3,2,1,0:T(8,128)(2,1)S(1)} %get-tuple-element.270), channel_id=1, source_target_pairs={{0,2},{1,3},{2,0},{3,1},{4,6},{5,7},{6,4},{7,5},{8,10},{9,11},{10,... | collective-permute-start | bytes 1769480 | tf_op jit(solution)/shard_map/ppermute | solution.py:526
  168.7 21.3 %collective-permute-start.35 = (bf16[2,2,2,2,96,384]{5,4,3,2,1,0:T(8,128)(2,1)}, bf16[2,2,2,2,96,384]{5,4,3,2,1,0:T(8,128)(2,1)}, u32[]{:S(2)}, u32[]{:S(2)}) collective-permute-start(bf16[2,2,2,2,96,384]{5,4,3,2,1,0:T(8,128)(2,1)} %bitcast.380), channel_id=1, source_target_pairs={{0,1},{1,0},{2,3},{3,2},{4,5},{5,4},{6,7},{7,6},{8,9},{9,8},{10,11... | collective-permute-start | bytes 3538952 | tf_op jit(solution)/shard_map/ppermute | solution.py:526
  170.8 16.9 %collective-permute-start.34 = (bf16[2,2,96,768]{3,2,1,0:T(8,128)(2,1)}, bf16[2,2,96,768]{3,2,1,0:T(8,128)(2,1)S(1)}, u32[]{:S(2)}, u32[]{:S(2)}) collective-permute-start(bf16[2,2,96,768]{3,2,1,0:T(8,128)(2,1)} %fusion.12), channel_id=1, source_target_pairs={{0,2},{1,3},{2,0},{3,1},{4,6},{5,7},{6,4},{7,5},{8,10},{9,11},{10,... | collective-permute-start | bytes 1769480 | tf_op jit(solution)/shard_map/ppermute | solution.py:526
  174.2 15.8 %collective-permute-start.33 = (bf16[2,2,96,768]{3,2,1,0:T(8,128)(2,1)}, bf16[2,2,96,768]{3,2,1,0:T(8,128)(2,1)}, u32[]{:S(2)}, u32[]{:S(2)}) collective-permute-start(bf16[2,2,96,768]{3,2,1,0:T(8,128)(2,1)} %fusion.18), channel_id=1, source_target_pairs={{0,4},{4,0},{8,12},{12,8},{16,20},{20,16},{24,28},{28,24},{1,5},{5... | collective-permute-start | bytes 1769480 | tf_op jit(solution)/shard_map/ppermute | solution.py:526
  187.2 3.4 %copy-start.32 = (bf16[384,768]{1,0:T(8,128)(2,1)S(1)}, bf16[384,768]{1,0:T(8,128)(2,1)}, u32[]{:S(2)}) copy-start(bf16[384,768]{1,0:T(8,128)(2,1)} %get-tuple-element.179) | copy-start | bytes 1769476
  187.7 4.4 %copy-start.19 = (bf16[2,2,96,768]{3,2,1,0:T(8,128)(2,1)}, bf16[2,2,96,768]{3,2,1,0:T(8,128)(2,1)S(1)}, u32[]{:S(2)}) copy-start(bf16[2,2,96,768]{3,2,1,0:T(8,128)(2,1)S(1)} %collective-permute-done.34) | copy-start | bytes 1769476
  190.0 15.0 %collective-permute-start.37 = (bf16[2,2,2,2,96,384]{5,4,3,2,1,0:T(8,128)(2,1)}, bf16[2,2,2,2,96,384]{5,4,3,2,1,0:T(8,128)(2,1)}, u32[]{:S(2)}, u32[]{:S(2)}) collective-permute-start(bf16[2,2,2,2,96,384]{5,4,3,2,1,0:T(8,128)(2,1)} %bitcast.73), channel_id=1, source_target_pairs={{0,1},{1,0},{2,3},{3,2},{4,5},{5,4},{6,7},{7,6},{8,9},{9,8},{10,11... | collective-permute-start | bytes 3538952 | tf_op jit(solution)/shard_map/ppermute | solution.py:526
  192.2 6.6 %copy-start.33 = (bf16[384,768]{1,0:T(8,128)(2,1)S(1)}, bf16[384,768]{1,0:T(8,128)(2,1)}, u32[]{:S(2)}) copy-start(bf16[384,768]{1,0:T(8,128)(2,1)} %get-tuple-element.181) | copy-start | bytes 1769476
  195.2 21.5 %all-to-all-start.1 = ((f32[32,1,288]{2,1,0:T(1,128)}), f32[32,1,288]{2,1,0:T(1,128)}, u32[]{:S(2)}, u32[]{:S(2)}) async-start(f32[32,1,288]{2,1,0:T(1,128)} %shard_map.261), calls=%async_computation.1 | async-start | bytes 98304 | tf_op jit(solution)/shard_map/all_to_all | solution.py:571
  201.7 15.8 %collective-permute-start.36 = (bf16[2,2,2,96,384]{4,3,2,1,0:T(8,128)(2,1)S(1)}, bf16[2,2,2,96,384]{4,3,2,1,0:T(8,128)(2,1)}, u32[]{:S(2)}, u32[]{:S(2)}) collective-permute-start(bf16[2,2,2,96,384]{4,3,2,1,0:T(8,128)(2,1)S(1)} %fusion.24), channel_id=1, source_target_pairs={{0,2},{1,3},{2,0},{3,1},{4,6},{5,7},{6,4},{7,5},{8,10},{9,11},{10,... | collective-permute-start | bytes 1769480 | tf_op jit(solution)/shard_map/ppermute | solution.py:526
  203.1 5.6 %copy-start.10 = (bf16[768,768]{1,0:T(8,128)(2,1)S(1)}, bf16[768,768]{1,0:T(8,128)(2,1)}, u32[]{:S(2)}) copy-start(bf16[768,768]{1,0:T(8,128)(2,1)} %get-tuple-element.137) | copy-start | bytes 3538948
  205.0 3.7 %copy-start.6 = (bf16[2,2,2,96,768]{4,3,2,1,0:T(8,128)(2,1)S(1)}, bf16[2,2,2,96,768]{4,3,2,1,0:T(8,128)(2,1)}, u32[]{:S(2)}) copy-start(bf16[2,2,2,96,768]{4,3,2,1,0:T(8,128)(2,1)} %copy-done.5) | copy-start | bytes 3538948
  205.0 3.7 %copy-start.20 = (bf16[2,2,96,768]{3,2,1,0:T(8,128)(2,1)S(1)}, bf16[2,2,96,768]{3,2,1,0:T(8,128)(2,1)}, u32[]{:S(2)}) copy-start(bf16[2,2,96,768]{3,2,1,0:T(8,128)(2,1)} %copy-done.19) | copy-start | bytes 1769476
  207.2 15.4 %collective-permute-start.38 = (bf16[2,2,2,96,384]{4,3,2,1,0:T(8,128)(2,1)}, bf16[2,2,2,96,384]{4,3,2,1,0:T(8,128)(2,1)}, u32[]{:S(2)}, u32[]{:S(2)}) collective-permute-start(bf16[2,2,2,96,384]{4,3,2,1,0:T(8,128)(2,1)} %fusion.25), channel_id=1, source_target_pairs={{0,4},{4,0},{8,12},{12,8},{16,20},{20,16},{24,28},{28,24},{1,5},{5... | collective-permute-start | bytes 1769480 | tf_op jit(solution)/shard_map/ppermute | solution.py:526
  210.8 21.2 %collective-permute-start.41 = (bf16[192,768]{1,0:T(8,128)(2,1)}, bf16[192,768]{1,0:T(8,128)(2,1)}, u32[]{:S(2)}, u32[]{:S(2)}) collective-permute-start(bf16[192,768]{1,0:T(8,128)(2,1)} %pad_maximum_fusion.13), channel_id=1, source_target_pairs={{0,16},{4,20},{8,24},{12,28},{16,0},{20,4},{24,8},{28,12},{1,17},{... | collective-permute-start | bytes 884744 | tf_op jit(solution)/shard_map/ppermute | solution.py:526
  214.0 18.0 %collective-permute-start.40 = (bf16[192,768]{1,0:T(8,128)(2,1)}, bf16[192,768]{1,0:T(8,128)(2,1)}, u32[]{:S(2)}, u32[]{:S(2)}) collective-permute-start(bf16[192,768]{1,0:T(8,128)(2,1)} %pad_maximum_fusion.12), channel_id=1, source_target_pairs={{0,8},{4,12},{8,0},{12,4},{16,24},{20,28},{24,16},{28,20},{1,9},{5... | collective-permute-start | bytes 884744 | tf_op jit(solution)/shard_map/ppermute | solution.py:526
  216.3 17.9 %collective-permute-start.39 = (bf16[192,768]{1,0:T(8,128)(2,1)}, bf16[192,768]{1,0:T(8,128)(2,1)}, u32[]{:S(2)}, u32[]{:S(2)}) collective-permute-start(bf16[192,768]{1,0:T(8,128)(2,1)} %pad_maximum_fusion.11), channel_id=1, source_target_pairs={{0,24},{4,28},{8,16},{12,20},{16,8},{20,12},{24,0},{28,4},{1,25},{... | collective-permute-start | bytes 884744 | tf_op jit(solution)/shard_map/ppermute | solution.py:526
  217.4 10.9 %copy-start.18 = (bf16[384,768]{1,0:T(8,128)(2,1)S(1)}, bf16[384,768]{1,0:T(8,128)(2,1)}, u32[]{:S(2)}) copy-start(bf16[384,768]{1,0:T(8,128)(2,1)} %fusion.9) | copy-start | bytes 1769476
  224.4 9.8 %collective-permute-start.43 = (bf16[2,2,96,384]{3,2,1,0:T(8,128)(2,1)}, bf16[2,2,96,384]{3,2,1,0:T(8,128)(2,1)}, u32[]{:S(2)}, u32[]{:S(2)}) collective-permute-start(bf16[2,2,96,384]{3,2,1,0:T(8,128)(2,1)} %fusion.29), channel_id=1, source_target_pairs={{0,2},{1,3},{2,0},{3,1},{4,6},{5,7},{6,4},{7,5},{8,10},{9,11},{10,... | collective-permute-start | bytes 884744 | tf_op jit(solution)/shard_map/ppermute | solution.py:526
  227.1 8.1 %collective-permute-start.42 = (bf16[2,2,96,384]{3,2,1,0:T(8,128)(2,1)}, bf16[2,2,96,384]{3,2,1,0:T(8,128)(2,1)}, u32[]{:S(2)}, u32[]{:S(2)}) collective-permute-start(bf16[2,2,96,384]{3,2,1,0:T(8,128)(2,1)} %fusion.30), channel_id=1, source_target_pairs={{0,4},{4,0},{8,12},{12,8},{16,20},{20,16},{24,28},{28,24},{1,5},{5... | collective-permute-start | bytes 884744 | tf_op jit(solution)/shard_map/ppermute | solution.py:526
  238.0 9.7 %collective-permute-start.44 = (bf16[96,768]{1,0:T(8,128)(2,1)S(1)}, bf16[96,768]{1,0:T(8,128)(2,1)S(1)}, u32[]{:S(2)}, u32[]{:S(2)}) collective-permute-start(bf16[96,768]{1,0:T(8,128)(2,1)S(1)} %pad_maximum_fusion.15), channel_id=1, source_target_pairs={{0,24},{4,28},{8,16},{12,20},{16,8},{20,12},{24,0},{28,4},{1,25},{... | collective-permute-start | bytes 442376 | tf_op jit(solution)/shard_map/ppermute | solution.py:526
  241.1 8.8 %collective-permute-start.45 = (bf16[96,768]{1,0:T(8,128)(2,1)S(1)}, bf16[96,768]{1,0:T(8,128)(2,1)S(1)}, u32[]{:S(2)}, u32[]{:S(2)}) collective-permute-start(bf16[96,768]{1,0:T(8,128)(2,1)S(1)} %pad_maximum_fusion.16), channel_id=1, source_target_pairs={{0,8},{4,12},{8,0},{12,4},{16,24},{20,28},{24,16},{28,20},{1,9},{5... | collective-permute-start | bytes 442376 | tf_op jit(solution)/shard_map/ppermute | solution.py:526
  245.5 9.7 %collective-permute-start.46 = (bf16[96,768]{1,0:T(8,128)(2,1)S(1)}, bf16[96,768]{1,0:T(8,128)(2,1)S(1)}, u32[]{:S(2)}, u32[]{:S(2)}) collective-permute-start(bf16[96,768]{1,0:T(8,128)(2,1)S(1)} %pad_maximum_fusion.17), channel_id=1, source_target_pairs={{0,16},{4,20},{8,24},{12,28},{16,0},{20,4},{24,8},{28,12},{1,17},{... | collective-permute-start | bytes 442376 | tf_op jit(solution)/shard_map/ppermute | solution.py:526
  (19 other events, 37.0 us)
